TPU v7x, 128 devices: a whole 4x4x4 slice. The times are simulated.
128 devices in a mesh: aa: 8 (over x, core), ba: 16 (over z, y).
Axes of the slice: x: 4, y: 4, z: 4, core: 2. Of those that a mesh axis runs over, the one named last changes fastest.
Arguments:
- head_outputs: bfloat16 [2048, 4096], P('ba'), may hold values from -6 to 6
- stream: bfloat16 [2048, 4096], P('ba'), may hold values from -6 to 6
- adapter_down_factors: bfloat16 [4096, 1024], P(None, 'aa'), may hold values from -0.09375 to 0.09375
- adapter_up_factors: bfloat16 [1024, 4096], P('aa'), may hold values from -1.5 to 1.5
- norm_gain_vector: float32 [4096], replicated, may hold values from 0.5 to 1.5
- router_matrix: bfloat16 [4096, 8], replicated, may hold values from -0.09375 to 0.09375
- token_adapter_index: int32 [2048], P('ba'), may hold values from 0 to 63
- token_expert_index: int32 [2048, 2], P('ba'), may hold values from 0 to 7, all different within a row; in each aligned block of 128 rows (0 to 127, 128 to 255, ...) at most 48 rows name the same one
- gate_weight: bfloat16 [16, 4096, 7168], P('ba', None, 'aa'), may hold values from -0.09375 to 0.09375
- up_weight: bfloat16 [16, 4096, 7168], P('ba', None, 'aa'), may hold values from -0.09375 to 0.09375
- down_weight: bfloat16 [16, 7168, 4096], P('ba', 'aa'), may hold values from -0.046875 to 0.046875
Outputs:
- mixed: bfloat16 [2048, 4096], P('ba', 'aa')
- adapter_load: float32 [64], P('aa')
Inputs may be any that keep to these rules, and one draw needn't show every extreme that they name: `token_expert_index`: the two experts of a row differ; in each aligned block of 128 rows no expert is named by more than 48 rows.
All inputs are finite; a program needn't handle non-finite values.
Results may differ from a plain program's by a relative error of at most 0.0049.
Values may be sent and summed in bfloat16 or wider, within the bound.
A program may use at most 128 MiB of HBM per device.

v0:
```python
import jax
import jax.numpy as jnp
from jax import lax
from jax.sharding import PartitionSpec as P

E = 8
ADAPTER_RANK = 16
CAP = 48


EPS = 1e-05
ADAPTER_SCALE = 2.0


def copy_for_each(array, axis):
    copies = jnp.broadcast_to(array, (lax.axis_size(axis), *array.shape))
    return lax.all_to_all(copies, axis, split_axis=0, concat_axis=0, tiled=True)


def taken_together(array, axis):
    everything = copy_for_each(array, axis)
    return jnp.sum(everything, axis=0)


def rows_for(lines, length):
    spare = -len(lines) % length
    return jnp.pad(lines, [(0, spare)] + [(0, 0)] * (lines.ndim - 1))


def sum_in_two_steps(array, axis):
    lines = array.reshape(-1, *array.shape[1:][-1:])
    own = lax.psum_scatter(
        rows_for(lines, lax.axis_size(axis)), axis, scatter_dimension=0, tiled=True
    )
    whole = lax.all_gather(own, axis).reshape(-1, *lines.shape[1:])
    return lax.slice_in_dim(whole, 0, len(lines)).reshape(array.shape)


def items_in_groups(array, axis, split_dim, concat_dim, work, item_dim, out_dim):
    items = jax.tree.leaves(array)[0].shape[item_dim]
    count = 2 if items % 2 == 0 else 1
    finished = []
    for k in range(count):
        group = jax.tree.map(
            lambda a: lax.slice_in_dim(
                a, k * (items // count), (k + 1) * (items // count), axis=item_dim
            ),
            array,
        )
        finished.append(
            work(
                lax.all_to_all(
                    group, axis, split_axis=split_dim, concat_axis=concat_dim, tiled=True
                )
            )
        )
    return jax.tree.map(lambda *parts: jnp.concatenate(parts, axis=out_dim), *finished)


def shards(
    head_outputs,
    stream,
    adapter_down_factors,
    adapter_up_factors,
    norm_gain_vector,
    router_matrix,
    token_adapter_index,
    token_expert_index,
    gate_weight,
    up_weight,
    down_weight,
):
    tok_rows = head_outputs.shape[0]
    model_width = head_outputs.shape[1]
    held_count = adapter_down_factors.shape[1] // ADAPTER_RANK
    groups = lax.axis_size("aa")
    index_aa = lax.axis_index("aa")
    local_ids = token_adapter_index - index_aa * held_count
    column_holder = jnp.arange(adapter_down_factors.shape[1], dtype=jnp.int32) // ADAPTER_RANK
    rank_projected = jnp.dot(head_outputs, adapter_down_factors, preferred_element_type=jnp.float32)
    rank_projected = jnp.where(
        local_ids[:, None] == column_holder[None, :], rank_projected, 0.0
    ).astype(jnp.bfloat16)
    partial_update = ADAPTER_SCALE * jnp.dot(
        rank_projected, adapter_up_factors, preferred_element_type=jnp.float32
    )
    tallies = jnp.sum(
        (local_ids[:, None] == jnp.arange(held_count, dtype=jnp.int32)[None, :]).astype(
            jnp.float32
        ),
        axis=0,
    )
    adapter_load = taken_together(tallies, "ba")
    share_width = model_width // groups
    adapter_update = sum_in_two_steps(partial_update, "aa")
    residual_stream = stream.astype(jnp.float32) + adapter_update
    inv_norm = lax.rsqrt(jnp.mean(residual_stream * residual_stream, axis=1, keepdims=True) + EPS)
    normed = (residual_stream * inv_norm * norm_gain_vector).astype(jnp.bfloat16)
    residual_share = lax.dynamic_slice_in_dim(
        residual_stream, index_aa * share_width, share_width, 1
    )
    logits = jnp.dot(normed, router_matrix, preferred_element_type=jnp.float32)
    experts_iota = jnp.arange(E, dtype=jnp.int32)
    chosen = (token_expert_index[:, :, None] == experts_iota[None, None, :]).astype(jnp.float32)
    picked = jnp.sum(chosen * logits[:, None, :], axis=2)
    weights = 1.0 / (1.0 + jnp.exp(picked[:, ::-1] - picked))
    flat_experts = token_expert_index.reshape(-1)
    expert_hits = (flat_experts[:, None] == experts_iota[None, :]).astype(jnp.int32)
    before = jnp.cumsum(expert_hits, axis=0) - expert_hits
    slot_index = flat_experts * CAP + jnp.sum(before * expert_hits, axis=1)
    slots_iota = jnp.arange(E * CAP, dtype=jnp.int32)
    placed = slot_index[None, :] == slots_iota[:, None]
    pick_rows = jnp.sum(placed.astype(jnp.float32).reshape(E * CAP, tok_rows, 2), axis=2).astype(
        jnp.bfloat16
    )
    outgoing = jnp.dot(pick_rows, normed, preferred_element_type=jnp.float32).astype(jnp.bfloat16)
    halves = lax.axis_size("ba") // E
    outgoing = jnp.repeat(outgoing.reshape(E, CAP, model_width), halves, axis=0)
    mixing = jnp.where(placed, weights.reshape(1, -1), 0.0)
    mixing = jnp.sum(mixing.reshape(E * CAP, tok_rows, 2), axis=2)

    def experts(received):
        sources = received.shape[0]
        items = received.shape[1]
        flat_rows = received.reshape(sources * items, model_width)
        gate_proj = jnp.dot(flat_rows, gate_weight[0], preferred_element_type=jnp.float32)
        up_proj = jnp.dot(flat_rows, up_weight[0], preferred_element_type=jnp.float32)
        hidden = (jax.nn.silu(gate_proj) * up_proj).astype(jnp.bfloat16)
        partial_value = jnp.dot(hidden, down_weight[0], preferred_element_type=jnp.float32).reshape(
            sources, items, model_width
        )
        reduced = lax.psum_scatter(partial_value, "aa", scatter_dimension=2, tiled=True)
        returned = lax.all_to_all(reduced, "ba", split_axis=0, concat_axis=0, tiled=True)
        return returned

    returned = items_in_groups(outgoing, "ba", 0, 0, experts, 1, 1)
    summed = jnp.sum(returned.reshape(E, halves, CAP, returned.shape[2]), axis=1).reshape(
        E * CAP, returned.shape[2]
    )
    gathered = jnp.einsum("sr,sd->rd", mixing, summed, precision=lax.Precision.HIGHEST)
    mixed_share = residual_share + gathered
    return (mixed_share.astype(jnp.bfloat16), adapter_load)


def solution(mesh):
    in_specs = (
        P("ba", None),
        P("ba", None),
        P(None, "aa"),
        P("aa", None),
        P(),
        P(),
        P("ba"),
        P("ba", None),
        P("ba", None, "aa"),
        P("ba", None, "aa"),
        P("ba", "aa", None),
    )
    out_specs = (P("ba", "aa"), P("aa"))
    return jax.shard_map(shards, mesh=mesh, in_specs=in_specs, out_specs=out_specs, check_vma=False)
```

profile of v0, /device:TPU:0, one launch (start us, length us, event | category | flops | bytes accessed | tf_op | source)
XLA Modules:
  0.0 268.0 jit_solution(243396699306617388)
XLA Ops:
  7.2 0.7 and_select_fusion
  8.0 0.4 copy-done
  8.4 3.7 %convolution_multiply_fusion = f32[128,4096]{1,0:T(8,128)} fusion(bf16[128,4096]{1,0:T(8,128)(2,1)S(1)} %copy-done, bf16[128,4096]{1,0:T(8,128)(2,1)} %param.11, bf16[4096,128]{1,0:T(8,128)(2,1)} %param.13, s32[128]{0:T(128)S(1)} %get-tuple-element.8, s32[128]{0:T(128)S(1)} %get-tuple-element.9), kind=kOutput, calls=%fused_computation.13 | convolution fusion | flops 269008896 | bytes 5243904 | tf_op jit(solution)/shard_map/dot_general | solution.py:84
  12.2 36.4 %reduce-scatter.4.cloned.1.call-done = f32[16,4096]{1,0:T(8,128)} async-done(((f32[128,4096]{1,0:T(8,128)}), f32[16,4096]{1,0:T(8,128)}) %reduce-scatter.4.cloned.1.call-update) | async-done | bytes 262160 | tf_op jit(solution)/shard_map/reduce_scatter | solution.py:32
  48.8 0.1 eq.86
  48.9 0.1 eq.82
  49.0 0.6 reduce-window.6
  49.6 0.2 slice_reduce_fusion
  50.0 0.1 reduce_sum.75
  50.2 24.3 %all-gather.3.cloned.1.call-done = f32[128,4096]{1,0:T(8,128)} async-done(((f32[16,4096]{1,0:T(8,128)}), f32[128,4096]{1,0:T(8,128)}) %all-gather.3.cloned.1.call-update) | async-done | bytes 2097168 | tf_op jit(solution)/shard_map/all_gather | solution.py:35
  74.5 2.0 multiply_reduce_fusion
  76.5 0.4 fusion.35
  77.1 1.0 convolution_convert_fusion
  78.2 0.8 broadcast_in_dim.19
  79.0 2.1 fusion.36
  81.1 47.0 %all_to_all.26 = bf16[16,24,4096]{2,1,0:T(8,128)(2,1)S(1)} all-to-all(bf16[16,24,4096]{2,1,0:T(8,128)(2,1)S(1)} %get-tuple-element.6), channel_id=1, replica_groups=mesh['aa'=8,'ba'=16] {'ba'}, dimensions={0} | all-to-all | bytes 6291456 | tf_op jit(solution)/shard_map/all_to_all | solution.py:52
  128.2 3.4 %fusion.10 = f32[384,896]{1,0:T(8,128)S(1)} fusion(bf16[384,4096]{1,0:T(8,128)(2,1)S(1)} %bitcast.56, bf16[1,4096,896]{2,1,0:T(8,128)(2,1)S(1)} %bitcast.62), kind=kOutput, calls=%fused_computation.10 | convolution fusion | flops 2818572288 | bytes 11862016 | tf_op jit(solution)/shard_map/dot_general | solution.py:126
  131.7 3.5 %fusion.21 = bf16[384,896]{1,0:T(8,128)(2,1)S(1)} fusion(bf16[384,4096]{1,0:T(8,128)(2,1)S(1)} %bitcast.57, bf16[1,4096,896]{2,1,0:T(8,128)(2,1)S(1)} %bitcast.64, f32[384,896]{1,0:T(8,128)S(1)} %fusion.10), kind=kOutput, calls=%fused_computation.22 | convolution fusion | flops 2820636672 | bytes 12550144 | tf_op jit(solution)/shard_map/dot_general | solution.py:127
  135.2 5.4 %fusion.2 = f32[16,24,4096]{2,1,0:T(8,128)} fusion(bf16[16,24,896]{2,1,0:T(8,128)(2,1)S(1)} %bitcast.71, bf16[1,896,4096]{2,1,0:T(8,128)(2,1)S(1)} %bitcast.68), kind=kOutput, calls=%fused_computation.2 | convolution fusion | flops 2818572288 | bytes 14319616 | tf_op jit(solution)/shard_map/dot_general | solution.py:129
  140.6 43.4 %all_to_all.27 = bf16[16,24,4096]{2,1,0:T(8,128)(2,1)S(1)} all-to-all(bf16[16,24,4096]{2,1,0:T(8,128)(2,1)} %get-tuple-element.7), channel_id=1, replica_groups=mesh['aa'=8,'ba'=16] {'ba'}, dimensions={0} | all-to-all | bytes 6291456 | tf_op jit(solution)/shard_map/all_to_all | solution.py:52
  184.0 5.8 %fusion.8 = f32[384,896]{1,0:T(8,128)S(1)} fusion(bf16[384,4096]{1,0:T(8,128)(2,1)S(1)} %bitcast.58, bf16[1,4096,896]{2,1,0:T(8,128)(2,1)} %param.19), kind=kOutput, calls=%fused_computation.8 | convolution fusion | flops 2818572288 | bytes 11862016 | tf_op jit(solution)/shard_map/dot_general | solution.py:126
  189.8 3.4 %fusion.18 = bf16[384,896]{1,0:T(8,128)(2,1)S(1)} fusion(bf16[384,4096]{1,0:T(8,128)(2,1)S(1)} %bitcast.59, bf16[1,4096,896]{2,1,0:T(8,128)(2,1)S(1)} %bitcast.66, f32[384,896]{1,0:T(8,128)S(1)} %fusion.8), kind=kOutput, calls=%fused_computation.21 | convolution fusion | flops 2820636672 | bytes 12550144 | tf_op jit(solution)/shard_map/dot_general | solution.py:127
  193.3 5.3 %fusion = f32[16,24,4096]{2,1,0:T(8,128)} fusion(bf16[16,24,896]{2,1,0:T(8,128)(2,1)S(1)} %bitcast.72, bf16[1,896,4096]{2,1,0:T(8,128)(2,1)S(1)} %bitcast.70), kind=kOutput, calls=%fused_computation | convolution fusion | flops 2818572288 | bytes 14319616 | tf_op jit(solution)/shard_map/dot_general | solution.py:129
  198.6 0.1 convert_reduce_fusion.1
  198.8 10.4 %all_to_all.28 = f32[16,1,8]{2,1,0:T(1,128)S(1)} all-to-all(f32[16,1,8]{2,1,0:T(1,128)S(1)} %broadcast_in_dim.38), channel_id=1, replica_groups=mesh['aa'=8,'ba'=16] {'ba'}, dimensions={0} | all-to-all | bytes 1024 | tf_op jit(solution)/shard_map/all_to_all | solution.py:17
  209.2 4.3 %all-to-all-start.1 = ((f32[16,24,512]{2,1,0:T(8,128)}), f32[16,24,512]{2,1,0:T(8,128)}, u32[]{:S(2)}, u32[]{:S(2)}) async-start(f32[16,24,512]{2,1,0:T(8,128)} %reduce-scatter.6.cloned.1.call-done), calls=%async_computation.3 | async-start | bytes 1572864 | tf_op jit(solution)/shard_map/all_to_all | solution.py:133
  213.5 24.2 %reduce-scatter.8.cloned.1.call-done = f32[16,24,512]{2,1,0:T(8,128)} async-done(((f32[16,24,4096]{2,1,0:T(8,128)}), f32[16,24,512]{2,1,0:T(8,128)}) %reduce-scatter.8.cloned.1.call-update) | async-done | bytes 786448 | tf_op jit(solution)/shard_map/reduce_scatter | solution.py:132
  237.7 7.3 %all-to-all-start.3 = ((f32[16,24,512]{2,1,0:T(8,128)}), f32[16,24,512]{2,1,0:T(8,128)}, u32[]{:S(2)}, u32[]{:S(2)}) async-start(f32[16,24,512]{2,1,0:T(8,128)} %reduce-scatter.8.cloned.1.call-done), calls=%async_computation.6 | async-start | bytes 1572864 | tf_op jit(solution)/shard_map/all_to_all | solution.py:133
  245.1 0.5 reduce_sum.82
  245.6 12.9 %all-to-all-done.3 = f32[16,24,512]{2,1,0:T(8,128)} async-done(((f32[16,24,512]{2,1,0:T(8,128)}), f32[16,24,512]{2,1,0:T(8,128)}, u32[]{:S(2)}, u32[]{:S(2)}) %all-to-all-start.3) | async-done | bytes 786464 | tf_op jit(solution)/shard_map/all_to_all | solution.py:133
  258.5 1.6 bitcast_reduce_fusion
  260.2 1.3 fusion.24
  (59 shorter events, 0.8 us)
Async XLA Ops:
  7.2 1.2 copy-start
  7.2 41.4 %reduce-scatter.4.cloned.1.call-start = ((), (), s32[]{:S(2)}) async-start(), calls=%async_computation.8 | async-start | bytes 2359296 | tf_op jit(solution)/shard_map/reduce_scatter | solution.py:32
  8.4 40.2 %copy-start.5 = (s32[128,2]{0,1:T(2,128)S(1)}, s32[128,2]{0,1:T(2,128)}, u32[]{:S(2)}) copy-start(s32[128,2]{0,1:T(2,128)} %param.18) | copy-start | bytes 3076
  12.1 62.4 %copy-start.2 = (bf16[128,4096]{1,0:T(8,128)(2,1)S(1)}, bf16[128,4096]{1,0:T(8,128)(2,1)}, u32[]{:S(2)}) copy-start(bf16[128,4096]{1,0:T(8,128)(2,1)} %param.12) | copy-start | bytes 3145732
  12.1 64.4 %copy-start.3 = (f32[4096]{0:T(1024)S(1)}, f32[4096]{0:T(1024)}, u32[]{:S(2)}) copy-start(f32[4096]{0:T(1024)} %param.15) | copy-start | bytes 49156
  12.1 64.4 %copy-start.4 = (bf16[4096,8]{0,1:T(8,128)(2,1)S(1)}, bf16[4096,8]{0,1:T(8,128)(2,1)}, u32[]{:S(2)}) copy-start(bf16[4096,8]{0,1:T(8,128)(2,1)} %param.16) | copy-start | bytes 196612
  12.1 62.3 %all-gather.3.cloned.1.call-start = ((), (), s32[]{:S(2)}) async-start(), calls=%async_computation.11 | async-start | bytes 2359296 | tf_op jit(solution)/shard_map/all_gather | solution.py:35
  48.6 160.6 %reduce-scatter.6.cloned.1.call-start = ((), (), s32[]{:S(2)}) async-start(), calls=%async_computation.9 | async-start | bytes 7077888 | tf_op jit(solution)/shard_map/reduce_scatter | solution.py:132
  78.2 50.0 %slice-start = ((s8[7340032]{0:T(1024)(128)(4,1)}), s8[3145728]{0:T(1024)(128)(4,1)S(1)}, s32[]{:S(2)}) async-start(s8[7340032]{0:T(1024)(128)(4,1)} %bitcast.61), calls=%async_computation.12 | async-start | bytes 6291456
  79.0 49.2 %slice-start.1 = ((s8[7340032]{0:T(1024)(128)(4,1)}), s8[4194304]{0:T(1024)(128)(4,1)S(1)}, s32[]{:S(2)}) async-start(s8[7340032]{0:T(1024)(128)(4,1)} %bitcast.61), calls=%async_computation.13 | async-start | bytes 8388608
  81.1 50.5 %slice-start.2 = ((s8[7340032]{0:T(1024)(128)(4,1)}), s8[4194304]{0:T(1024)(128)(4,1)S(1)}, s32[]{:S(2)}) async-start(s8[7340032]{0:T(1024)(128)(4,1)} %bitcast.63), calls=%async_computation.14 | async-start | bytes 8388608
  81.1 54.0 %slice-start.6 = ((s8[7340032]{0:T(1024)(128)(4,1)}), s8[3145728]{0:T(1024)(128)(4,1)S(1)}, s32[]{:S(2)}) async-start(s8[7340032]{0:T(1024)(128)(4,1)} %bitcast.67), calls=%async_computation.18 | async-start | bytes 6291456
  128.2 3.5 %slice-start.3 = ((s8[7340032]{0:T(1024)(128)(4,1)}), s8[3145728]{0:T(1024)(128)(4,1)S(1)}, s32[]{:S(2)}) async-start(s8[7340032]{0:T(1024)(128)(4,1)} %bitcast.63), calls=%async_computation.15 | async-start | bytes 6291456
  128.2 7.0 %slice-start.7 = ((s8[7340032]{0:T(1024)(128)(4,1)}), s8[4194304]{0:T(1024)(128)(4,1)S(1)}, s32[]{:S(2)}) async-start(s8[7340032]{0:T(1024)(128)(4,1)} %bitcast.67), calls=%async_computation.19 | async-start | bytes 8388608
  140.6 97.2 %reduce-scatter.8.cloned.1.call-start = ((), (), s32[]{:S(2)}) async-start(), calls=%async_computation.10 | async-start | bytes 7077888 | tf_op jit(solution)/shard_map/reduce_scatter | solution.py:132
  140.6 49.2 %slice-start.4 = ((s8[7340032]{0:T(1024)(128)(4,1)}), s8[4194304]{0:T(1024)(128)(4,1)S(1)}, s32[]{:S(2)}) async-start(s8[7340032]{0:T(1024)(128)(4,1)} %bitcast.65), calls=%async_computation.16 | async-start | bytes 8388608
  140.6 52.6 %slice-start.8 = ((s8[7340032]{0:T(1024)(128)(4,1)}), s8[4194304]{0:T(1024)(128)(4,1)S(1)}, s32[]{:S(2)}) async-start(s8[7340032]{0:T(1024)(128)(4,1)} %bitcast.69), calls=%async_computation.20 | async-start | bytes 8388608
  184.0 5.8 %slice-start.5 = ((s8[7340032]{0:T(1024)(128)(4,1)}), s8[3145728]{0:T(1024)(128)(4,1)S(1)}, s32[]{:S(2)}) async-start(s8[7340032]{0:T(1024)(128)(4,1)} %bitcast.65), calls=%async_computation.17 | async-start | bytes 6291456
  184.0 9.3 %slice-start.9 = ((s8[7340032]{0:T(1024)(128)(4,1)}), s8[3145728]{0:T(1024)(128)(4,1)S(1)}, s32[]{:S(2)}) async-start(s8[7340032]{0:T(1024)(128)(4,1)} %bitcast.69), calls=%async_computation.21 | async-start | bytes 6291456
  198.8 62.7 %copy-start.1 = (bf16[128,4096]{1,0:T(8,128)(2,1)S(1)}, bf16[128,4096]{1,0:T(8,128)(2,1)}, u32[]{:S(2)}) copy-start(bf16[128,4096]{1,0:T(8,128)(2,1)} %param.14) | copy-start | bytes 3145732
  209.2 28.5 %all-to-all-start.1 = ((f32[16,24,512]{2,1,0:T(8,128)}), f32[16,24,512]{2,1,0:T(8,128)}, u32[]{:S(2)}, u32[]{:S(2)}) async-start(f32[16,24,512]{2,1,0:T(8,128)} %reduce-scatter.6.cloned.1.call-done), calls=%async_computation.3 | async-start | bytes 1572864 | tf_op jit(solution)/shard_map/all_to_all | solution.py:133
  237.7 20.8 %all-to-all-start.3 = ((f32[16,24,512]{2,1,0:T(8,128)}), f32[16,24,512]{2,1,0:T(8,128)}, u32[]{:S(2)}, u32[]{:S(2)}) async-start(f32[16,24,512]{2,1,0:T(8,128)} %reduce-scatter.8.cloned.1.call-done), calls=%async_computation.6 | async-start | bytes 1572864 | tf_op jit(solution)/shard_map/all_to_all | solution.py:133
Sparse Core Ops, SparseCore 0:
  12.2 36.2 reduce-scatter.3
  50.3 24.1 all-gather.2
  140.7 39.1 reduce-scatter.5
  198.8 38.9 reduce-scatter.7
where the time goes:
time: 269 us; the launch traced here: 268 us
  blocking collectives  101 us (38%)
  waiting for transfers between devices  97.9 us (36%)
  matrix products  33.3 us (12%)
  between operations  14.1 us (5%)
  starting transfers between devices  11.8 us (4%)
  other arithmetic  5.87 us (2%)
  local copies, waits for them, and re-layouts  4.29 us (2%)
    all_to_all x2, blocking collectives, items_in_groups(): lax.all_to_all(group, axis, split_axis=split_dim, concat_axis=concat_dim,...  90.4 us
    reduce_scatter x1, waiting for transfers between devices, sum_in_two_steps(): lax.psum_scatter(rows_for(lines, lax.axis_size(axis)), axis, scatter_dime...  36.4 us
    all_gather x1, waiting for transfers between devices, sum_in_two_steps(): whole = lax.all_gather(own, axis).reshape(-1, *lines.shape[1:])  24.3 us
    reduce_scatter x2, waiting for transfers between devices, experts(): lax.psum_scatter(partial_value, 'aa', scatter_dimension=2, tiled=True)  24.2 us
    all_to_all x2, waiting for transfers between devices, experts(): lax.all_to_all(reduced, 'ba', split_axis=0, concat_axis=0, tiled=True)  12.9 us
    all_to_all x2, starting transfers between devices, experts(): lax.all_to_all(reduced, 'ba', split_axis=0, concat_axis=0, tiled=True)  11.6 us
    dot_general x2, matrix products, experts(): jnp.dot(hidden, down_weight[0], preferred_element_type=jnp.float32)  10.7 us
    all_to_all x1, blocking collectives, copy_for_each(): return lax.all_to_all(copies, axis, split_axis=0, concat_axis=0, tiled=True)  10.4 us
  transfers between devices with their start and end apart: 6, of which 4 were waited for; matrix products, arithmetic and copies ran while one was open for 6% of the time, Pallas kernels for 0%

commit v1 on v0

v1 whole, which is shorter than its diff:
```python
import jax
import jax.numpy as jnp
from jax import lax
from jax.experimental import pallas as pl
from jax.experimental.pallas import tpu as pltpu
from jax.sharding import PartitionSpec as P

MESH = pl.DeviceIdType.MESH
E = 8
RANK = 16
TOK = 128
DIM = 4096
FFD = 896
CH = 3
CR = 16
ROWS = 256
SL = 512
NT = FFD // 128
EPS = 1e-05
F32 = jnp.float32
BF16 = jnp.bfloat16


def place_of(f):
    x, core = f // 2, f % 2
    return core * 4 + (x % 2) * 2 + x // 2


def tdot(a, b):
    return lax.dot_general(a, b, (((0,), (0,)), ((), ())), preferred_element_type=F32)


def ntdot(a, b):
    return lax.dot_general(a, b, (((1,), (1,)), ((), ())), preferred_element_type=F32)


def kernel(
    head_h, stream_h, down_h, up_h, gain_ref, router_ref, idrow_ref, idcol_ref, ex_ref,
    g_h, u_h, d_h,
    out_ref, cnt_ref,
    head_v, down_v, stream_v, wgu, dv, upc, lows, low_own, stats, stat_own, lgs, lg_own, ids,
    nrm, outb, xb, hid, ysend, yrecv, yown, town, zsend, zrecv, rb, ret, mx, fsend, frecv, resid,
    load_sem, wsem, up_s, up_r, low_s, low_r, st_s, st_r, lg_s, lg_r, id_s, id_r,
    n_s, n_r, a_s, a_r, x_s, x_r, d_s, d_r, y_s, y_r, z_s, z_r, b_s, b_r, f_s, f_r,
):
    aa = lax.axis_index("aa")
    ba = lax.axis_index("ba")
    core, x = aa % 2, aa // 2
    xp, xh = x % 2, x // 2
    z, y = ba // 4, ba % 4

    def aa_at(dx, dc):
        return ((x + dx) % 4) * 2 + (core + dc) % 2

    def ba_at(d):
        return ((z + d // 4) % 4) * 4 + (y + d % 4) % 4

    def ba_from(d):
        return ((z + 4 - d // 4) % 4) * 4 + (y + 4 - d % 4) % 4

    def rcopy(src, dst, ss, rs, a, b):
        return pltpu.make_async_remote_copy(
            src_ref=src, dst_ref=dst, send_sem=ss, recv_sem=rs, device_id=(a, b),
            device_id_type=MESH,
        )

    def cols(i, width):
        return pl.ds(pl.multiple_of(i * width, width), width)

    loads = [
        pltpu.make_async_copy(head_h, head_v, load_sem.at[0]),
        pltpu.make_async_copy(down_h, down_v, load_sem.at[1]),
        pltpu.make_async_copy(stream_h.at[:, cols(aa, SL)], stream_v, load_sem.at[2]),
    ]
    for c in loads:
        c.start()

    barrier = pltpu.get_barrier_semaphore()
    for k in range(1, 8):
        pl.semaphore_signal(
            barrier, inc=1, device_id=(aa_at(k // 2, k % 2), ba), device_id_type=MESH
        )

    def greet(d, carry):
        pl.semaphore_signal(barrier, inc=1, device_id=(aa, ba_at(d)), device_id_type=MESH)
        return carry

    lax.fori_loop(1, 16, greet, 0)
    pl.semaphore_wait(barrier, 22)

    ups = []
    for k in range(1, 8):
        to = aa_at(k // 2, k % 2)
        ups.append(
            rcopy(up_h.at[:, cols(to, SL)], upc.at[k], up_s.at[k], up_r.at[k], to, ba)
        )
    for c in ups:
        c.start()
    own_up = pltpu.make_async_copy(up_h.at[:, cols(aa, SL)], upc.at[0], load_sem.at[3])
    own_up.start()

    def id_copy(d):
        return rcopy(idrow_ref, ids.at[d], id_s.at[d], id_r.at[d], aa, ba_at(d))

    def send_ids(d, carry):
        id_copy(d).start()
        return carry

    lax.fori_loop(1, 16, send_ids, 0)
    ids[0] = idrow_ref[...]

    def load_w(n, carry):
        for f in range(8):
            p = place_of(f)
            for half, w in enumerate((g_h, u_h)):
                pltpu.make_async_copy(
                    w.at[f * SL : (f + 1) * SL, cols(n, 128)],
                    wgu.at[n, p * SL : (p + 1) * SL, half * 128 : (half + 1) * 128],
                    wsem.at[0],
                ).start()
        return carry

    lax.fori_loop(0, NT, load_w, 0)
    for f in range(8):
        pltpu.make_async_copy(
            d_h.at[:, f * SL : (f + 1) * SL], dv.at[place_of(f)], wsem.at[1]
        ).start()

    for c in loads[:2]:
        c.wait()
    rank = jnp.dot(head_v[...], down_v[...], preferred_element_type=F32)
    lane = lax.broadcasted_iota(jnp.int32, (TOK, 128), 1)
    sub = lax.broadcasted_iota(jnp.int32, (TOK, 128), 0)
    idcol = idcol_ref[...]
    rank = jnp.where(idcol == aa * 8 + lane // RANK, rank, 0.0).astype(BF16)
    fold = (
        lax.broadcasted_iota(jnp.int32, (RANK, 128), 1) % RANK
        == lax.broadcasted_iota(jnp.int32, (RANK, 128), 0)
    ).astype(BF16)
    mine = ntdot(fold, rank)
    low_own[...] = mine.astype(BF16)
    lowc = []
    for k in range(1, 8):
        lowc.append(
            rcopy(low_own, lows.at[k], low_s.at[k], low_r.at[k], aa_at(k // 2, k % 2), ba)
        )
    for c in lowc:
        c.start()

    ex0, ex1 = ex_ref[0:1, :], ex_ref[1:2, :]
    e_sub = lax.broadcasted_iota(jnp.int32, (E, TOK), 0)
    hit0, hit1 = ex0 == e_sub, ex1 == e_sub
    hit = hit0 | hit1
    earlier = (sub < lane).astype(BF16)
    pos = jnp.dot(hit.astype(BF16), earlier, preferred_element_type=F32)
    pos = jnp.where(hit, pos, -1.0)
    posx = jnp.concatenate(
        [jnp.broadcast_to(pos[e : e + 1, :], (CR, TOK)) for e in range(E)], axis=0
    )
    row16 = (sub % CR).astype(F32)

    low = mine
    for k in range(1, 8):
        lowc[k - 1].wait_recv()
        low = low + lows[k].astype(F32)
    spread = tdot(low.astype(BF16), fold)

    own_up.wait()
    delta = jnp.zeros((TOK, SL), F32)
    for k in range(8):
        if k:
            ups[k - 1].wait_recv()
        src = aa_at(4 - k // 2, k % 2)
        lowk = jnp.where(idcol == src * 8 + lane // RANK, spread, 0.0).astype(BF16)
        delta = delta + jnp.dot(lowk, upc[k], preferred_element_type=F32)
    loads[2].wait()
    res = stream_v[...].astype(F32) + 2.0 * delta
    resid[...] = res
    sq = jnp.sum(res * res, axis=1, keepdims=True)
    stat_own[...] = jnp.transpose(jnp.broadcast_to(sq, (TOK, 128)))[0:8, :]
    stc = []
    for k in range(1, 8):
        stc.append(
            rcopy(stat_own, stats.at[k], st_s.at[k], st_r.at[k], aa_at(k // 2, k % 2), ba)
        )
    for c in stc:
        c.start()
    total = stat_own[...]
    for k in range(1, 8):
        stc[k - 1].wait_recv()
        total = total + stats[k]
    inv = lax.rsqrt(total[0:1, :] * (1.0 / DIM) + EPS)
    inv = jnp.transpose(jnp.broadcast_to(inv, (128, TOK)))[:, 0:1]
    own_n = (resid[...] * inv * gain_ref[:, cols(aa, SL)]).astype(BF16)
    nrm[xh] = own_n
    opp = aa_at(2, 0)
    ncopy = rcopy(nrm.at[xh], nrm.at[xh], n_s.at[0], n_r.at[0], opp, ba)
    ncopy.start()

    lg_own[...] = ntdot(router_ref[:, cols(aa, SL)], own_n)
    lgc = []
    for k in range(1, 8):
        lgc.append(
            rcopy(lg_own, lgs.at[k], lg_s.at[k], lg_r.at[k], aa_at(k // 2, k % 2), ba)
        )
    for c in lgc:
        c.start()

    grp = core * 2 + xp
    picks = [(posx == row16 + float(CR * c)).astype(BF16) for c in range(CH)]
    for c in range(CH):
        outb[c, :, cols(xh, SL)] = jnp.dot(
            picks[c], own_n, preferred_element_type=F32
        ).astype(BF16)
    ncopy.wait_recv()

    def a_copy(c, d):
        to = ba_at(d)
        return rcopy(
            outb.at[c, cols(to // 2, CR), :],
            xb.at[c, cols(ba, CR), cols(grp, 2 * SL)],
            a_s.at[c, d], a_r.at[c, d], aa, to,
        )

    for c in range(CH):
        outb[c, :, cols(1 - xh, SL)] = jnp.dot(
            picks[c], nrm[1 - xh], preferred_element_type=F32
        ).astype(BF16)

        def send_a(d, carry, c=c):
            a_copy(c, d).start()
            return carry

        lax.fori_loop(1, 16, send_a, 0)
        xb[c, cols(ba, CR), cols(grp, 2 * SL)] = outb[c, cols(ba // 2, CR), :]

    sib = aa_at(0, 1)
    place = core * 4 + xp * 2 + xh
    xc, dc1, dc2 = [], [], []
    for c in range(CH):
        sl = xb.at[c, :, cols(place, SL)]
        xc.append(
            [
                rcopy(sl, sl, x_s.at[c, 0], x_r.at[c, 0], aa_at(1, 0), ba),
                rcopy(sl, sl, x_s.at[c, 1], x_r.at[c, 1], aa_at(3, 0), ba),
            ]
        )
        g1 = xb.at[c, :, cols(grp, 2 * SL)]
        g2 = xb.at[c, :, cols(core * 2 + 1 - xp, 2 * SL)]
        dc1.append(rcopy(g1, g1, d_s.at[c, 0], d_r.at[c, 0], sib, ba))
        dc2.append(rcopy(g2, g2, d_s.at[c, 1], d_r.at[c, 1], sib, ba))

    def arrive(c):
        def wait_a(d, carry):
            a_copy(c, d).wait_recv()
            return carry

        lax.fori_loop(1, 16, wait_a, 0)
        for k in xc[c]:
            k.start()
        dc1[c].start()

    def relay(c):
        for k in xc[c]:
            k.wait_recv()
        dc2[c].start()

    def ready(c):
        dc1[c].wait_recv()
        dc2[c].wait_recv()

    def gate_up(c):
        def step(n, carry):
            gu = jnp.dot(xb[c], wgu[n], preferred_element_type=F32)
            g, u = gu[:, :128], gu[:, 128:]
            hid[:, cols(n, 128)] = (g / (1.0 + jnp.exp(-g)) * u).astype(BF16)
            return carry

        lax.fori_loop(0, NT, step, 0)

    def y_copy(c, j):
        return rcopy(ysend.at[c, j], yrecv.at[c, j], y_s.at[c, j], y_r.at[c, j], sib, ba)

    def project(c):
        def step_far(j, carry):
            ysend[c, j] = jnp.dot(
                hid[...], dv[(1 - core) * 4 + j], preferred_element_type=F32
            ).astype(BF16)
            y_copy(c, j).start()
            return carry

        lax.fori_loop(0, 4, step_far, 0)

        def step_own(j, carry):
            yown[j] = jnp.dot(hid[...], dv[core * 4 + j], preferred_element_type=F32)
            return carry

        lax.fori_loop(0, 4, step_own, 0)

    def spot(dx):
        xx = (x + dx) % 4
        return (xx % 2) * 2 + xx // 2

    zc = [
        [
            rcopy(zsend.at[c, 0], zrecv.at[c, 0], z_s.at[c, 0], z_r.at[c, 0], aa_at(1, 0), ba),
            rcopy(zsend.at[c, 1], zrecv.at[c, 1], z_s.at[c, 1], z_r.at[c, 1], aa_at(3, 0), ba),
        ]
        for c in range(CH)
    ]

    def pair_sum(c, j):
        return yown[j] + yrecv[c, j].astype(F32)

    def reduce_cores(c):
        def wait_y(j, carry):
            y_copy(c, j).wait_recv()
            return carry

        lax.fori_loop(0, 4, wait_y, 0)
        for i, dx in enumerate((1, 3)):
            zsend[c, i] = pair_sum(c, spot(dx)).astype(BF16)
            zc[c][i].start()
        rb[c, :, cols(1 - xh, SL)] = pair_sum(c, spot(2)).astype(BF16)
        town[...] = pair_sum(c, spot(0))

    def b_copy(c, d):
        to = ba_at(d)
        return rcopy(
            rb.at[c, cols(to, CR), :], ret.at[c, cols(ba, CR), :],
            b_s.at[c, d], b_r.at[c, d], aa, to,
        )

    def reduce_chips(c):
        zc[c][0].wait_recv()
        zc[c][1].wait_recv()
        rb[c, :, cols(xh, SL)] = (
            town[...] + zrecv[c, 0].astype(F32) + zrecv[c, 1].astype(F32)
        ).astype(BF16)

        def send_b(d, carry):
            b_copy(c, d).start()
            return carry

        lax.fori_loop(1, 16, send_b, 0)
        ret[c, cols(ba, CR), :] = rb[c, cols(ba, CR), :]

    def mix_weights():
        lg = lg_own[...]
        for k in range(1, 8):
            lgc[k - 1].wait_recv()
            lg = lg + lgs[k]
        l0 = jnp.sum(jnp.where(hit0, lg, 0.0), axis=0, keepdims=True)
        l1 = jnp.sum(jnp.where(hit1, lg, 0.0), axis=0, keepdims=True)
        w0 = 1.0 / (1.0 + jnp.exp(l1 - l0))
        w1 = 1.0 / (1.0 + jnp.exp(l0 - l1))
        return jnp.where(hit0, w0, 0.0) + jnp.where(hit1, w1, 0.0)

    def mix(c, wx):
        def wait_b(d, carry):
            b_copy(c, d).wait_recv()
            return carry

        lax.fori_loop(1, 16, wait_b, 0)
        w = jnp.where(posx == row16 + float(CR * c), wx, 0.0)
        hi = w.astype(BF16)
        lo = (w - hi.astype(F32)).astype(BF16)
        both = jnp.concatenate([hi, lo], axis=1)
        both = jnp.concatenate(
            [both[(s // 2) * CR : (s // 2 + 1) * CR, :] for s in range(2 * E)], axis=0
        )
        got = tdot(both, ret[c])
        got = got[:TOK, :] + got[TOK:, :]
        if c == 0:
            mx[...] = got
        else:
            mx[...] += got

    arrive(0)
    relay(0)
    arrive(1)
    ready(0)
    pltpu.make_async_copy(wgu, wgu, wsem.at[0]).wait()
    gate_up(0)
    relay(1)
    arrive(2)
    pltpu.make_async_copy(dv, dv, wsem.at[1]).wait()
    project(0)
    ready(1)
    gate_up(1)
    relay(2)
    reduce_cores(0)
    project(1)
    reduce_chips(0)
    ready(2)
    gate_up(2)
    reduce_cores(1)
    project(2)
    reduce_chips(1)
    wt = mix_weights()
    wx = jnp.concatenate(
        [jnp.broadcast_to(wt[e : e + 1, :], (CR, TOK)) for e in range(E)], axis=0
    )
    reduce_cores(2)
    mix(0, wx)
    reduce_chips(2)

    def count(d, acc):
        @pl.when(d > 0)
        def _():
            id_copy(d).wait_recv()

        row = jnp.broadcast_to(ids[d], (8, TOK))
        want = aa * 8 + lax.broadcasted_iota(jnp.int32, (8, TOK), 0)
        return acc + (row == want).astype(F32)

    tally = lax.fori_loop(0, 16, count, jnp.zeros((8, TOK), F32))
    cnt_ref[...] = jnp.broadcast_to(jnp.sum(tally, axis=1, keepdims=True), (8, TOK))

    mix(1, wx)
    mix(2, wx)
    fsend[...] = mx[:, cols(1 - xh, SL)].astype(BF16)
    fcopy = rcopy(fsend, frecv, f_s.at[0], f_r.at[0], opp, ba)
    fcopy.start()
    base = resid[...] + mx[:, cols(xh, SL)]
    fcopy.wait_recv()
    out_ref[...] = (base + frecv[...].astype(F32)).astype(BF16)

    for c in ups + lowc + stc + lgc + [ncopy, fcopy]:
        c.wait_send()

    def drain(d, carry):
        id_copy(d).wait_send()
        for c in range(CH):
            a_copy(c, d).wait_send()
            b_copy(c, d).wait_send()
        return carry

    lax.fori_loop(1, 16, drain, 0)
    for c in range(CH):
        for k in xc[c] + zc[c] + [dc1[c], dc2[c]]:
            k.wait_send()

        def drain_y(j, carry, c=c):
            y_copy(c, j).wait_send()
            return carry

        lax.fori_loop(0, 4, drain_y, 0)


def shards(
    head_outputs, stream, adapter_down_factors, adapter_up_factors, norm_gain_vector,
    router_matrix, token_adapter_index, token_expert_index, gate_weight, up_weight, down_weight,
):
    any_spec = pl.BlockSpec(memory_space=pl.ANY)
    vmem = pl.BlockSpec(memory_space=pltpu.VMEM)
    V = pltpu.VMEM
    S = pltpu.SemaphoreType.DMA
    mixed, load = pl.pallas_call(
        kernel,
        out_shape=(
            jax.ShapeDtypeStruct((TOK, SL), BF16),
            jax.ShapeDtypeStruct((8, TOK), F32),
        ),
        in_specs=[any_spec] * 4 + [vmem] * 5 + [any_spec] * 3,
        out_specs=(vmem, vmem),
        scratch_shapes=[
            V((TOK, DIM), BF16),
            V((DIM, 128), BF16),
            V((TOK, SL), BF16),
            V((NT, DIM, 256), BF16),
            V((8, FFD, SL), BF16),
            V((8, 128, SL), BF16),
            V((8, RANK, TOK), BF16),
            V((RANK, TOK), BF16),
            V((8, 8, TOK), F32),
            V((8, TOK), F32),
            V((8, E, TOK), F32),
            V((E, TOK), F32),
            V((16, 1, TOK), jnp.int32),
            V((2, TOK, SL), BF16),
            V((CH, E * CR, 2 * SL), BF16),
            V((CH, ROWS, DIM), BF16),
            V((ROWS, FFD), BF16),
            V((CH, 4, ROWS, SL), BF16),
            V((CH, 4, ROWS, SL), BF16),
            V((4, ROWS, SL), F32),
            V((ROWS, SL), F32),
            V((CH, 2, ROWS, SL), BF16),
            V((CH, 2, ROWS, SL), BF16),
            V((CH, ROWS, 2 * SL), BF16),
            V((CH, ROWS, 2 * SL), BF16),
            V((TOK, 2 * SL), F32),
            V((TOK, SL), BF16),
            V((TOK, SL), BF16),
            V((TOK, SL), F32),
            S((4,)), S((2,)),
            S((8,)), S((8,)), S((8,)), S((8,)), S((8,)), S((8,)), S((8,)), S((8,)),
            S((16,)), S((16,)),
            S((1,)), S((1,)),
            S((CH, 16)), S((CH, 16)),
            S((CH, 2)), S((CH, 2)), S((CH, 2)), S((CH, 2)),
            S((CH, 4)), S((CH, 4)),
            S((CH, 2)), S((CH, 2)),
            S((CH, 16)), S((CH, 16)),
            S((1,)), S((1,)),
        ],
        compiler_params=pltpu.CompilerParams(
            collective_id=0, has_side_effects=True, vmem_limit_bytes=66_000_000
        ),
    )(
        head_outputs, stream, adapter_down_factors, adapter_up_factors,
        norm_gain_vector.reshape(1, DIM), router_matrix.T,
        token_adapter_index.reshape(1, TOK), token_adapter_index.reshape(TOK, 1),
        token_expert_index.T, gate_weight[0], up_weight[0], down_weight[0],
    )
    return mixed, load[:, 0]


def solution(mesh):
    in_specs = (
        P("ba", None), P("ba", None), P(None, "aa"), P("aa", None), P(), P(), P("ba"),
        P("ba", None), P("ba", None, "aa"), P("ba", None, "aa"), P("ba", "aa", None),
    )
    out_specs = (P("ba", "aa"), P("aa"))
    return jax.shard_map(shards, mesh=mesh, in_specs=in_specs, out_specs=out_specs, check_vma=False)
```

time: 269 us -> 118 us (0.44)
  Pallas kernels: 0 us -> 113 us
  blocking collectives: 101 us -> 0 us
  waiting for transfers between devices: 97.9 us -> 0 us
  matrix products: 33.3 us -> 0 us
  between operations: 14.1 us -> 0.64 us
  starting transfers between devices: 11.8 us -> 0 us
  other arithmetic: 5.87 us -> 0 us
    pallas_call x0 -> x1, Pallas kernels: none -> 113 us  [shards(): pl.pallas_call(kernel, out_shape=(jax.ShapeDtypeStruct((TOK, SL), BF16),...]
    all_to_all x3 -> x0, blocking collectives: 101 us -> none  [the longest x2 90.4 us: items_in_groups(): lax.all_to_all(group, axis, split_axis=split_dim, concat_axis=concat_dim,...]
    reduce_scatter x3 -> x0, waiting for transfers between devices: 60.6 us -> none  [the longest x1 36.4 us: sum_in_two_steps(): lax.psum_scatter(rows_for(lines, lax.axis_size(axis)), axis, scatter_dime...]
    dot_general x10 -> x0, matrix products: 33.3 us -> none  [the longest x2 10.7 us: experts(): jnp.dot(hidden, down_weight[0], preferred_element_type=jnp.float32)]
    all_gather x1 -> x0, waiting for transfers between devices: 24.3 us -> none  [sum_in_two_steps(): whole = lax.all_gather(own, axis).reshape(-1, *lines.shape[1:])]
    all_to_all x2 -> x0, waiting for transfers between devices: 12.9 us -> none  [experts(): lax.all_to_all(reduced, 'ba', split_axis=0, concat_axis=0, tiled=True)]
    all_to_all x2 -> x0, starting transfers between devices: 11.6 us -> none  [experts(): lax.all_to_all(reduced, 'ba', split_axis=0, concat_axis=0, tiled=True)]
    reduce_sum x7 -> x0, other arithmetic: 4.48 us -> none  [the longest x1 1.99 us: shards(): jnp.mean(residual_stream * residual_stream, axis=1, keepdims=True) + EPS]
  transfers between devices with their start and end apart: 6 -> 0, of which waited for: 4 -> 0; matrix products, arithmetic and copies ran while one was open for 6% -> 0% of each run, Pallas kernels for 0% -> 0%
where the time goes in v1:
time: 118 us
  Pallas kernels  113 us (96%)
  local copies, waits for them, and re-layouts  4.26 us (4%)
    pallas_call x1, Pallas kernels, shards(): pl.pallas_call(kernel, out_shape=(jax.ShapeDtypeStruct((TOK, SL), BF16),...  113 us

profile of v1, /device:TPU:0, one launch (start us, length us, event | category | flops | bytes accessed | tf_op | source)
XLA Modules:
  0.0 117.7 jit_solution(2123113873267036558)
XLA Ops:
  0.6 1.4 %copy.14.idcol_ref = s32[128,1]{1,0:T(8,128)} copy(s32[128,1]{0,1:T(1,128)} %bitcast.13) | data formatting | bytes 1024 | tf_op jit(solution)/shard_map/reshape | solution.py:514
  2.0 112.8 %shard_map.122 = (bf16[128,512]{1,0:T(8,128)(2,1)}, f32[8,128]{1,0:T(8,128)}) custom-call(bf16[128,4096]{1,0:T(8,128)(2,1)} %head_h.1, bf16[128,4096]{1,0:T(8,128)(2,1)} %stream_h.1, bf16[4096,128]{1,0:T(8,128)(2,1)} %down_h.1, bf16[128,4096]{1,0:T(8,128)(2,1)} %up_h.1, f32[1,4096]{1,0:T(1,128)} %bitcast.12, bf16[8,4096]{1,0:T(8,128)(2,1)} %bitcast.11, ...), custom_call_target="tpu_custom_call" | custom-call | tf_op jit(solution)/shard_map/pallas_call | solution.py:459
  114.8 1.3 %slice_reduce_fusion = f32[8]{0:T(128)} fusion(f32[8,128]{1,0:T(8,128)} %get-tuple-element.5), kind=kLoop, calls=%fused_computation | loop fusion | bytes 64 | tf_op jit(solution)/shard_map/slice | solution.py:517
  116.1 1.6 %copy.16 = bf16[128,512]{1,0:T(8,128)(2,1)} copy(bf16[128,512]{1,0:T(8,128)(2,1)} %get-tuple-element.8) | data formatting | bytes 262144

commit v2 on v1

v2 whole, which is shorter than its diff:
```python
import jax
import jax.numpy as jnp
from jax import lax
from jax.experimental import pallas as pl
from jax.experimental.pallas import tpu as pltpu
from jax.sharding import PartitionSpec as P

MESH = pl.DeviceIdType.MESH
E = 8
RANK = 16
TOK = 128
DIM = 4096
FFD = 896
CH = 3
CR = 16
ROWS = 256
SL = 512
NT = FFD // 128
EPS = 1e-05
F32 = jnp.float32
BF16 = jnp.bfloat16


def place_of(f):
    x, core = f // 2, f % 2
    return core * 4 + (x % 2) * 2 + x // 2


def tdot(a, b):
    return lax.dot_general(a, b, (((0,), (0,)), ((), ())), preferred_element_type=F32)


def ntdot(a, b):
    return lax.dot_general(a, b, (((1,), (1,)), ((), ())), preferred_element_type=F32)


def kernel(
    head_h, stream_h, down_h, up_h, gain_ref, router_ref, idrow_ref, idcol_ref, ex_ref,
    g_h, u_h, d_h,
    out_ref, cnt_ref,
    head_v, down_v, up_v, stream_v, wgu, dv, lsend, lrecv, tsend, trecv, stats, stat_own,
    lgs, lg_own, ids, rout, routes, scl,
    nrm, outb, xb, hid, ysend, yrecv, town, zsend, zrecv, rb, ret, mx, fsend, frecv, resid,
    load_sem, wsem, l_s, l_r, t_s, t_r, st_s, st_r, lg_s, lg_r, id_s, id_r, rt_s, rt_r,
    n_s, n_r, a_s, a_r, o_s, o_r, x_s, x_r, d_s, d_r, y_s, y_r, z_s, z_r,
    b_s, b_r, q_s, q_r, f_s, f_r,
):
    aa = lax.axis_index("aa")
    ba = lax.axis_index("ba")
    core, x = aa % 2, aa // 2
    xp, xh = x % 2, x // 2
    z, y = ba // 4, ba % 4

    def aa_at(dx, dc):
        return ((x + dx) % 4) * 2 + (core + dc) % 2

    def ba_at(d):
        return ((z + d // 4) % 4) * 4 + (y + d % 4) % 4

    def ba_from(d):
        return ((z + 4 - d // 4) % 4) * 4 + (y + 4 - d % 4) % 4

    def rcopy(src, dst, ss, rs, a, b):
        return pltpu.make_async_remote_copy(
            src_ref=src, dst_ref=dst, send_sem=ss, recv_sem=rs, device_id=(a, b),
            device_id_type=MESH,
        )

    def cols(i, width):
        return pl.ds(pl.multiple_of(i * width, width), width)

    def each_peer(body):
        def step(d, carry):
            body(d)
            return carry

        lax.fori_loop(1, 16, step, 0)

    sib = aa_at(0, 1)
    opp = aa_at(2, 0)

    loads = [
        pltpu.make_async_copy(head_h, head_v, load_sem.at[0]),
        pltpu.make_async_copy(down_h, down_v, load_sem.at[1]),
        pltpu.make_async_copy(up_h, up_v, load_sem.at[2]),
        pltpu.make_async_copy(stream_h.at[:, cols(aa, SL)], stream_v, load_sem.at[3]),
    ]
    for c in loads:
        c.start()

    barrier = pltpu.get_barrier_semaphore()
    for k in range(1, 8):
        pl.semaphore_signal(
            barrier, inc=1, device_id=(aa_at(k // 2, k % 2), ba), device_id_type=MESH
        )
    each_peer(
        lambda d: pl.semaphore_signal(
            barrier, inc=1, device_id=(aa, ba_at(d)), device_id_type=MESH
        )
    )

    lane = lax.broadcasted_iota(jnp.int32, (TOK, 128), 1)
    sub = lax.broadcasted_iota(jnp.int32, (TOK, 128), 0)
    loads[0].wait()
    loads[1].wait()
    rank = jnp.dot(head_v[...], down_v[...], preferred_element_type=F32)
    rank = jnp.where(idcol_ref[...] == aa * 8 + lane // RANK, rank, 0.0).astype(BF16)
    loads[2].wait()

    def load_w(n, carry):
        for f in range(8):
            p = place_of(f)
            for half, w in enumerate((g_h, u_h)):
                pltpu.make_async_copy(
                    w.at[f * SL : (f + 1) * SL, cols(n, 128)],
                    wgu.at[n, p * SL : (p + 1) * SL, half * 128 : (half + 1) * 128],
                    wsem.at[0],
                ).start()
        return carry

    lax.fori_loop(0, NT, load_w, 0)
    for f in range(8):
        pltpu.make_async_copy(
            d_h.at[:, f * SL : (f + 1) * SL], dv.at[place_of(f)], wsem.at[1]
        ).start()

    def term(dx, dc):
        part = up_v[:, cols(aa_at(dx, dc), SL)]
        return 2.0 * jnp.dot(rank, part, preferred_element_type=F32)

    ORDER = (2, 1, 3, 0)
    for dx in ORDER:
        lsend[dx] = term(dx, 1).astype(BF16)

    pl.semaphore_wait(barrier, 22)
    lc = [rcopy(lsend.at[i], lrecv.at[i], l_s.at[i], l_r.at[i], sib, ba) for i in range(4)]
    tc = [
        rcopy(tsend.at[i], trecv.at[i], t_s.at[i], t_r.at[i], aa_at(i, 0), ba)
        for i in range(1, 4)
    ]
    for dx in ORDER:
        lc[dx].start()

    ex0, ex1 = ex_ref[0:1, :], ex_ref[1:2, :]
    e_sub = lax.broadcasted_iota(jnp.int32, (E, TOK), 0)
    hit0, hit1 = ex0 == e_sub, ex1 == e_sub
    hit = hit0 | hit1
    earlier = (sub < lane).astype(BF16)
    pos = jnp.dot(hit.astype(BF16), earlier, preferred_element_type=F32)
    pos = jnp.where(hit, pos, -1.0)
    posx = jnp.concatenate(
        [jnp.broadcast_to(pos[e : e + 1, :], (CR, TOK)) for e in range(E)], axis=0
    )
    row16 = (sub % CR).astype(F32)
    picks = [(posx == row16 + float(CR * c)).astype(BF16) for c in range(CH)]

    own_term = None
    for dx in ORDER:
        t = term(dx, 0)
        lc[dx].wait_recv()
        t = t + lrecv[dx].astype(F32)
        if dx:
            tsend[dx] = t.astype(BF16)
            tc[dx - 1].start()
        else:
            own_term = t

    def id_copy(d):
        return rcopy(idrow_ref, ids.at[d], id_s.at[d], id_r.at[d], aa, ba_at(d))

    each_peer(lambda d: id_copy(d).start())
    ids[0] = idrow_ref[...]

    loads[3].wait()
    res = stream_v[...].astype(F32) + own_term
    for c in (1, 3, 2):
        tc[c - 1].wait_recv()
        res = res + trecv[c].astype(F32)
    resid[...] = res
    gain = gain_ref[:, cols(aa, SL)]
    sq = jnp.sum(res * res, axis=1, keepdims=True)
    stat_own[...] = jnp.transpose(jnp.broadcast_to(sq, (TOK, 128)))[0:8, :]
    stc = [
        rcopy(stat_own, stats.at[k], st_s.at[k], st_r.at[k], aa_at(k // 2, k % 2), ba)
        for k in range(1, 8)
    ]
    for c in stc:
        c.start()
    own_n = (res * gain).astype(BF16)
    nrm[xh] = own_n
    ncopy = rcopy(nrm.at[xh], nrm.at[xh], n_s.at[0], n_r.at[0], opp, ba)
    ncopy.start()

    grp = core * 2 + xp

    def a_copy(c, d):
        to = ba_at(d)
        return rcopy(
            outb.at[c, cols(to // 2, CR), cols(xh, SL)],
            xb.at[c, cols(ba, CR), cols(grp * 2 + xh, SL)],
            a_s.at[c, d], a_r.at[c, d], aa, to,
        )

    def o_copy(c, d):
        to = ba_at(d)
        return rcopy(
            outb.at[c, cols(to // 2, CR), cols(1 - xh, SL)],
            xb.at[c, cols(ba, CR), cols(grp * 2 + 1 - xh, SL)],
            o_s.at[c, d], o_r.at[c, d], aa, to,
        )

    def send_rows(c, copy, half):
        outb[c, :, cols(half, SL)] = jnp.dot(
            picks[c], nrm[half], preferred_element_type=F32
        ).astype(BF16)
        each_peer(lambda d: copy(c, d).start())
        xb[c, cols(ba, CR), cols(grp * 2 + half, SL)] = outb[
            c, cols(ba // 2, CR), cols(half, SL)
        ]

    send_rows(0, a_copy, xh)
    total = stat_own[...]
    for k in range(1, 8):
        stc[k - 1].wait_recv()
        total = total + stats[k]
    inv_row = lax.rsqrt(total * (1.0 / DIM) + EPS)

    e_row = lax.broadcasted_iota(jnp.int32, (8, TOK), 0)
    for e in range(E):
        rout[e] = jnp.where(e_row == 0, jnp.broadcast_to(pos[e : e + 1, :], (8, TOK)), inv_row)

    def rt_copy(d):
        to = ba_at(d)
        return rcopy(rout.at[to // 2], routes.at[ba], rt_s.at[d], rt_r.at[d], aa, to)

    def rt_wait(d):
        src = ba_from(d)
        return rcopy(rout.at[0], routes.at[src], rt_s.at[d], rt_r.at[d], aa, src)

    each_peer(lambda d: rt_copy(d).start())
    routes[ba] = rout[ba // 2]
    send_rows(1, a_copy, xh)
    send_rows(2, a_copy, xh)

    place = core * 4 + xp * 2 + xh
    xc, dc = [], []
    for c in range(CH):
        own = xb.at[c, :, cols(place, SL)]
        far = xb.at[c, :, cols(core * 4 + xp * 2 + 1 - xh, SL)]
        near = xb.at[c, :, cols(core * 2 + 1 - xp, 2 * SL)]
        xc.append(
            [
                rcopy(own, own, x_s.at[c, 0], x_r.at[c, 0], aa_at(1, 0), ba),
                rcopy(own, own, x_s.at[c, 1], x_r.at[c, 1], aa_at(3, 0), ba),
            ]
        )
        dc.append(
            [
                rcopy(r, r, d_s.at[c, i], d_r.at[c, i], sib, ba)
                for i, r in enumerate((own, far, near))
            ]
        )

    def arrive_own(c):
        each_peer(lambda d: a_copy(c, d).wait_recv())
        for k in xc[c]:
            k.start()
        dc[c][0].start()

    def arrive_opp(c):
        each_peer(lambda d: o_copy(c, d).wait_recv())
        dc[c][1].start()

    def relay(c):
        for k in xc[c]:
            k.wait_recv()
        dc[c][2].start()

    def ready(c):
        for k in dc[c]:
            k.wait_recv()
        for s in range(16):
            r = routes[s]
            at = lax.broadcasted_iota(jnp.int32, (CR, TOK), 0).astype(F32) + float(CR * c)
            v = jnp.where(at == r[0:1, :], r[1:2, :], 0.0)
            scl[s * CR : (s + 1) * CR, :] = jnp.broadcast_to(
                jnp.sum(v, axis=1, keepdims=True), (CR, 128)
            )

    def gate_up(c):
        for n in range(NT):
            gu = jnp.dot(xb[c], wgu[n], preferred_element_type=F32)
            g, u = gu[:, :128] * scl[...], gu[:, 128:] * scl[...]
            hid[:, n * 128 : (n + 1) * 128] = (g / (1.0 + jnp.exp(-g)) * u).astype(BF16)

    zc = [
        {
            dx: rcopy(
                zsend.at[c, dx // 2], zrecv.at[c, dx // 2], z_s.at[c, dx // 2],
                z_r.at[c, dx // 2], aa_at(dx, 0), ba,
            )
            for dx in (1, 3)
        }
        for c in range(CH)
    ]
    yc = [
        [rcopy(ysend.at[c, i], yrecv.at[c, i], y_s.at[c, i], y_r.at[c, i], sib, ba) for i in range(4)]
        for c in range(CH)
    ]

    def spot(dx):
        xx = (x + dx) % 4
        return (xx % 2) * 2 + xx // 2

    def b_copy(c, d):
        to = ba_at(d)
        return rcopy(
            rb.at[c, cols(to, CR), cols(xh, SL)], ret.at[c, cols(ba, CR), cols(xh, SL)],
            b_s.at[c, d], b_r.at[c, d], aa, to,
        )

    def q_copy(c, d):
        to = ba_at(d)
        return rcopy(
            rb.at[c, cols(to, CR), cols(1 - xh, SL)], ret.at[c, cols(ba, CR), cols(1 - xh, SL)],
            q_s.at[c, d], q_r.at[c, d], aa, to,
        )

    def keep_own(c, half):
        ret[c, cols(ba, CR), cols(half, SL)] = rb[c, cols(ba, CR), cols(half, SL)]

    def project(c):
        for dx in (1, 3, 2, 0):
            ysend[c, dx] = jnp.dot(
                hid[...], dv[(1 - core) * 4 + spot(dx)], preferred_element_type=F32
            ).astype(BF16)
            yc[c][dx].start()
        for dx in (1, 3, 2, 0):
            v = jnp.dot(hid[...], dv[core * 4 + spot(dx)], preferred_element_type=F32)
            yc[c][dx].wait_recv()
            v = v + yrecv[c, dx].astype(F32)
            if dx == 0:
                town[c] = v
            elif dx == 2:
                rb[c, :, cols(1 - xh, SL)] = v.astype(BF16)
                each_peer(lambda d: q_copy(c, d).start())
                keep_own(c, 1 - xh)
            else:
                zsend[c, dx // 2] = v.astype(BF16)
                zc[c][dx].start()

    def reduce_chips(c):
        zc[c][1].wait_recv()
        zc[c][3].wait_recv()
        rb[c, :, cols(xh, SL)] = (
            town[c] + zrecv[c, 0].astype(F32) + zrecv[c, 1].astype(F32)
        ).astype(BF16)
        each_peer(lambda d: b_copy(c, d).start())
        keep_own(c, xh)

    def mix_weights():
        lg = lg_own[...]
        for k in range(1, 8):
            lgc[k - 1].wait_recv()
            lg = lg + lgs[k]
        l0 = jnp.sum(jnp.where(hit0, lg, 0.0), axis=0, keepdims=True)
        l1 = jnp.sum(jnp.where(hit1, lg, 0.0), axis=0, keepdims=True)
        w0 = 1.0 / (1.0 + jnp.exp(l1 - l0))
        w1 = 1.0 / (1.0 + jnp.exp(l0 - l1))
        return jnp.where(hit0, w0, 0.0) + jnp.where(hit1, w1, 0.0)

    def mix(c, wx, copy, half):
        each_peer(lambda d: copy(c, d).wait_recv())
        w = jnp.where(posx == row16 + float(CR * c), wx, 0.0)
        hi = w.astype(BF16)
        lo = (w - hi.astype(F32)).astype(BF16)
        both = jnp.concatenate([hi, lo], axis=1)
        both = jnp.concatenate(
            [both[(s // 2) * CR : (s // 2 + 1) * CR, :] for s in range(2 * E)], axis=0
        )
        got = tdot(both, ret[c, :, cols(half, SL)])
        got = got[:TOK, :] + got[TOK:, :]
        if c == 0:
            mx[half] = got
        else:
            mx[half] += got

    arrive_own(0)
    ncopy.wait_recv()
    for c in range(CH):
        send_rows(c, o_copy, 1 - xh)
    inv = jnp.transpose(jnp.broadcast_to(inv_row[0:1, :], (128, TOK)))[:, 0:1]
    normed = (resid[...] * inv * gain).astype(BF16)
    lg_own[...] = ntdot(router_ref[:, cols(aa, SL)], normed)
    lgc = [
        rcopy(lg_own, lgs.at[k], lg_s.at[k], lg_r.at[k], aa_at(k // 2, k % 2), ba)
        for k in range(1, 8)
    ]
    for c in lgc:
        c.start()
    arrive_own(1)
    relay(0)
    arrive_opp(0)
    arrive_own(2)
    each_peer(lambda d: rt_wait(d).wait_recv())
    ready(0)
    pltpu.make_async_copy(wgu, wgu, wsem.at[0]).wait()
    gate_up(0)
    relay(1)
    arrive_opp(1)
    pltpu.make_async_copy(dv, dv, wsem.at[1]).wait()
    project(0)
    ready(1)
    gate_up(1)
    relay(2)
    arrive_opp(2)
    reduce_chips(0)
    project(1)
    ready(2)
    gate_up(2)
    reduce_chips(1)
    wt = mix_weights()
    wx = jnp.concatenate(
        [jnp.broadcast_to(wt[e : e + 1, :], (CR, TOK)) for e in range(E)], axis=0
    )
    project(2)
    mix(0, wx, q_copy, 1 - xh)
    mix(0, wx, b_copy, xh)
    mix(1, wx, q_copy, 1 - xh)

    each_peer(lambda d: id_copy(d).wait_recv())
    want = aa * 8 + lax.broadcasted_iota(jnp.int32, (8, TOK), 0)
    tally = jnp.zeros((8, TOK), F32)
    for d in range(16):
        tally = tally + (jnp.broadcast_to(ids[d], (8, TOK)) == want).astype(F32)
    cnt_ref[...] = jnp.broadcast_to(jnp.sum(tally, axis=1, keepdims=True), (8, TOK))

    mix(2, wx, q_copy, 1 - xh)
    fsend[...] = mx[1 - xh].astype(BF16)
    fcopy = rcopy(fsend, frecv, f_s.at[0], f_r.at[0], opp, ba)
    fcopy.start()
    reduce_chips(2)
    mix(1, wx, b_copy, xh)
    mix(2, wx, b_copy, xh)
    base = resid[...] + mx[xh]
    fcopy.wait_recv()
    out_ref[...] = (base + frecv[...].astype(F32)).astype(BF16)

    for c in lc + tc + stc + lgc + [ncopy, fcopy]:
        c.wait_send()

    def drain(d):
        id_copy(d).wait_send()
        rt_copy(d).wait_send()
        for c in range(CH):
            for copy in (a_copy, o_copy, b_copy, q_copy):
                copy(c, d).wait_send()

    each_peer(drain)
    for c in range(CH):
        for k in xc[c] + list(zc[c].values()) + dc[c] + yc[c]:
            k.wait_send()


def shards(
    head_outputs, stream, adapter_down_factors, adapter_up_factors, norm_gain_vector,
    router_matrix, token_adapter_index, token_expert_index, gate_weight, up_weight, down_weight,
):
    any_spec = pl.BlockSpec(memory_space=pl.ANY)
    vmem = pl.BlockSpec(memory_space=pltpu.VMEM)
    V = pltpu.VMEM
    S = pltpu.SemaphoreType.DMA
    mixed, load = pl.pallas_call(
        kernel,
        out_shape=(
            jax.ShapeDtypeStruct((TOK, SL), BF16),
            jax.ShapeDtypeStruct((8, TOK), F32),
        ),
        in_specs=[any_spec] * 4 + [vmem] * 5 + [any_spec] * 3,
        out_specs=(vmem, vmem),
        scratch_shapes=[
            V((TOK, DIM), BF16),
            V((DIM, 128), BF16),
            V((128, DIM), BF16),
            V((TOK, SL), BF16),
            V((NT, DIM, 256), BF16),
            V((8, FFD, SL), BF16),
            V((4, TOK, SL), BF16),
            V((4, TOK, SL), BF16),
            V((4, TOK, SL), BF16),
            V((4, TOK, SL), BF16),
            V((8, 8, TOK), F32),
            V((8, TOK), F32),
            V((8, E, TOK), F32),
            V((E, TOK), F32),
            V((16, 1, TOK), jnp.int32),
            V((E, 8, TOK), F32),
            V((16, 8, TOK), F32),
            V((ROWS, 128), F32),
            V((2, TOK, SL), BF16),
            V((CH, E * CR, 2 * SL), BF16),
            V((CH, ROWS, DIM), BF16),
            V((ROWS, FFD), BF16),
            V((CH, 4, ROWS, SL), BF16),
            V((CH, 4, ROWS, SL), BF16),
            V((CH, ROWS, SL), F32),
            V((CH, 2, ROWS, SL), BF16),
            V((CH, 2, ROWS, SL), BF16),
            V((CH, ROWS, 2 * SL), BF16),
            V((CH, ROWS, 2 * SL), BF16),
            V((2, TOK, SL), F32),
            V((TOK, SL), BF16),
            V((TOK, SL), BF16),
            V((TOK, SL), F32),
            S((4,)), S((2,)),
            S((4,)), S((4,)), S((4,)), S((4,)), S((8,)), S((8,)), S((8,)), S((8,)),
            S((16,)), S((16,)), S((16,)), S((16,)),
            S((1,)), S((1,)),
            S((CH, 16)), S((CH, 16)), S((CH, 16)), S((CH, 16)),
            S((CH, 2)), S((CH, 2)), S((CH, 3)), S((CH, 3)),
            S((CH, 4)), S((CH, 4)),
            S((CH, 2)), S((CH, 2)),
            S((CH, 16)), S((CH, 16)), S((CH, 16)), S((CH, 16)),
            S((1,)), S((1,)),
        ],
        compiler_params=pltpu.CompilerParams(
            collective_id=0, has_side_effects=True, vmem_limit_bytes=66_000_000
        ),
    )(
        head_outputs, stream, adapter_down_factors, adapter_up_factors,
        norm_gain_vector.reshape(1, DIM), router_matrix.T,
        token_adapter_index.reshape(1, TOK), token_adapter_index.reshape(TOK, 1),
        token_expert_index.T, gate_weight[0], up_weight[0], down_weight[0],
    )
    return mixed, load[:, 0]


def solution(mesh):
    in_specs = (
        P("ba", None), P("ba", None), P(None, "aa"), P("aa", None), P(), P(), P("ba"),
        P("ba", None), P("ba", None, "aa"), P("ba", None, "aa"), P("ba", "aa", None),
    )
    out_specs = (P("ba", "aa"), P("aa"))
    return jax.shard_map(shards, mesh=mesh, in_specs=in_specs, out_specs=out_specs, check_vma=False)
```

time: 118 us -> 97.5 us (0.83)
  Pallas kernels: 113 us -> 92.3 us
    pallas_call x1, Pallas kernels: 113 us -> 92.3 us  [shards(): pl.pallas_call(kernel, out_shape=(jax.ShapeDtypeStruct((TOK, SL), BF16),...]
where the time goes in v2:
time: 97.5 us; the launch traced here: 97.2 us
  Pallas kernels  92.3 us (95%)
  local copies, waits for them, and re-layouts  4.26 us (4%)
    pallas_call x1, Pallas kernels, shards(): pl.pallas_call(kernel, out_shape=(jax.ShapeDtypeStruct((TOK, SL), BF16),...  92.3 us

profile of v2, /device:TPU:0, one launch (start us, length us, event | category | flops | bytes accessed | tf_op | source)
XLA Modules:
  0.0 97.2 jit_solution(16129945724039430115)
XLA Ops:
  0.6 1.4 %copy.14.idcol_ref = s32[128,1]{1,0:T(8,128)} copy(s32[128,1]{0,1:T(1,128)} %bitcast.13) | data formatting | bytes 1024 | tf_op jit(solution)/shard_map/reshape | solution.py:532
  2.0 92.3 %shard_map.122 = (bf16[128,512]{1,0:T(8,128)(2,1)}, f32[8,128]{1,0:T(8,128)}) custom-call(bf16[128,4096]{1,0:T(8,128)(2,1)} %head_h.1, bf16[128,4096]{1,0:T(8,128)(2,1)} %stream_h.1, bf16[4096,128]{1,0:T(8,128)(2,1)} %down_h.1, bf16[128,4096]{1,0:T(8,128)(2,1)} %up_h.1, f32[1,4096]{1,0:T(1,128)} %bitcast.12, bf16[8,4096]{1,0:T(8,128)(2,1)} %bitcast.11, ...), custom_call_target="tpu_custom_call" | custom-call | tf_op jit(solution)/shard_map/pallas_call | solution.py:473
  94.4 1.3 %slice_reduce_fusion = f32[8]{0:T(128)} fusion(f32[8,128]{1,0:T(8,128)} %get-tuple-element.5), kind=kLoop, calls=%fused_computation | loop fusion | bytes 64 | tf_op jit(solution)/shard_map/slice | solution.py:535
  95.7 1.6 %copy.16 = bf16[128,512]{1,0:T(8,128)(2,1)} copy(bf16[128,512]{1,0:T(8,128)(2,1)} %get-tuple-element.8) | data formatting | bytes 262144

commit v3 on v2

v3 whole, which is shorter than its diff:
```python
import jax
import jax.numpy as jnp
from jax import lax
from jax.experimental import pallas as pl
from jax.experimental.pallas import tpu as pltpu
from jax.sharding import PartitionSpec as P

MESH = pl.DeviceIdType.MESH
E = 8
RANK = 16
TOK = 128
DIM = 4096
FFD = 896
CH = 3
CR = 16
ROWS = 256
SL = 512
NT = FFD // 128
EPS = 1e-05
F32 = jnp.float32
BF16 = jnp.bfloat16


def place_of(f):
    x, core = f // 2, f % 2
    return (x % 2) * 4 + core * 2 + x // 2


def tdot(a, b):
    return lax.dot_general(a, b, (((0,), (0,)), ((), ())), preferred_element_type=F32)


def ntdot(a, b):
    return lax.dot_general(a, b, (((1,), (1,)), ((), ())), preferred_element_type=F32)


def kernel(
    head_h, stream_h, down_h, up_h, gain_h, router_h, idrow_h, ex_h,
    g_h, u_h, d_h,
    out_ref, cnt_ref,
    head_v, down_v, up_v, stream_v, gain_ref, router_ref, idrow_ref, ex_ref, wgu, dv, lsend, lrecv, tsend, trecv, stats, stat_own,
    lgs, lg_own, ids, rout, routes, scl,
    nrm, outb, xb, hid, ysend, yrecv, near, town, zsend, zrecv, rb, ret, mx, fsend, frecv, resid, acc,
    load_sem, wsem, l_s, l_r, t_s, t_r, st_s, st_r, lg_s, lg_r, id_s, id_r, rt_s, rt_r,
    n_s, n_r, a_s, a_r, x_s, x_r, d_s, d_r, y_s, y_r, z_s, z_r,
    b_s, b_r, f_s, f_r,
):
    aa = lax.axis_index("aa")
    ba = lax.axis_index("ba")
    rem, div = lax.rem, lax.div
    core, x = rem(aa, 2), div(aa, 2)
    xp, xh = rem(x, 2), div(x, 2)
    z, y = div(ba, 4), rem(ba, 4)

    def aa_at(dx, dc):
        return rem(x + dx, 4) * 2 + rem(core + dc, 2)

    def ba_at(d):
        return rem(z + div(d, 4), 4) * 4 + rem(y + rem(d, 4), 4)

    def take(ref, sem):
        pltpu.make_async_copy(ref, ref, sem).wait()

    def rcopy(src, dst, ss, rs, a, b):
        return pltpu.make_async_remote_copy(
            src_ref=src, dst_ref=dst, send_sem=ss, recv_sem=rs, device_id=(a, b),
            device_id_type=MESH,
        )

    def cols(i, width):
        return pl.ds(pl.multiple_of(i * width, width), width)

    def each_peer(body):
        def step(d, carry):
            body(d)
            return carry

        lax.fori_loop(1, 16, step, 0)

    sib = aa_at(0, 1)
    opp = aa_at(2, 0)

    loads = [
        pltpu.make_async_copy(head_h, head_v, load_sem.at[0]),
        pltpu.make_async_copy(down_h, down_v, load_sem.at[1]),
        pltpu.make_async_copy(up_h, up_v, load_sem.at[2]),
        pltpu.make_async_copy(idrow_h, idrow_ref, load_sem.at[4]),
        pltpu.make_async_copy(stream_h.at[:, cols(aa, SL)], stream_v, load_sem.at[3]),
        pltpu.make_async_copy(gain_h.at[:, cols(aa, SL)], gain_ref, load_sem.at[5]),
        pltpu.make_async_copy(router_h.at[:, cols(aa, SL)], router_ref, load_sem.at[6]),
        pltpu.make_async_copy(ex_h, ex_ref, load_sem.at[7]),
    ]
    for c in loads:
        c.start()

    barrier = pltpu.get_barrier_semaphore()
    for k in range(1, 8):
        pl.semaphore_signal(
            barrier, inc=1, device_id=(aa_at(k // 2, k % 2), ba), device_id_type=MESH
        )
    each_peer(
        lambda d: pl.semaphore_signal(
            barrier, inc=1, device_id=(aa, ba_at(d)), device_id_type=MESH
        )
    )

    lane = lax.broadcasted_iota(jnp.int32, (TOK, 128), 1)
    sub = lax.broadcasted_iota(jnp.int32, (TOK, 128), 0)
    loads[0].wait()
    loads[1].wait()
    loads[3].wait()
    rank = jnp.dot(head_v[...], down_v[...], preferred_element_type=F32)
    idcol = jnp.transpose(jnp.broadcast_to(idrow_ref[...].astype(F32), (128, TOK)))
    rank = jnp.where(idcol == (aa * 8 + lane // RANK).astype(F32), rank, 0.0).astype(BF16)
    loads[2].wait()

    def load_w(n, carry):
        for f in range(8):
            p = place_of(f)
            for half, w in enumerate((g_h, u_h)):
                pltpu.make_async_copy(
                    w.at[f * SL : (f + 1) * SL, cols(n, 128)],
                    wgu.at[n, p * SL : (p + 1) * SL, half * 128 : (half + 1) * 128],
                    wsem.at[0],
                ).start()
        return carry

    lax.fori_loop(0, NT, load_w, 0)
    for f in range(8):
        pltpu.make_async_copy(
            d_h.at[:, f * SL : (f + 1) * SL],
            dv.at[place_of(f) // 2, :, (place_of(f) % 2) * SL : (place_of(f) % 2 + 1) * SL],
            wsem.at[1],
        ).start()

    def term(dx, dc):
        part = up_v[:, cols(aa_at(dx, dc), SL)]
        return 2.0 * jnp.dot(rank, part, preferred_element_type=F32)

    ORDER = (2, 1, 3, 0)
    for dx in ORDER:
        lsend[dx] = term(dx, 1).astype(BF16)

    pl.semaphore_wait(barrier, 22)
    lc = [rcopy(lsend.at[i], lrecv.at[i], l_s.at[i], l_r.at[i], sib, ba) for i in range(4)]
    tc = [
        rcopy(tsend.at[i], trecv.at[i], t_s.at[i], t_r.at[i], aa_at(i, 0), ba)
        for i in range(1, 4)
    ]
    for dx in ORDER:
        lc[dx].start()

    loads[7].wait()
    ex0, ex1 = ex_ref[0:1, :], ex_ref[1:2, :]
    e_sub = lax.broadcasted_iota(jnp.int32, (E, TOK), 0)
    hit0, hit1 = ex0 == e_sub, ex1 == e_sub
    hit = hit0 | hit1
    earlier = (sub < lane).astype(BF16)
    pos = jnp.dot(hit.astype(BF16), earlier, preferred_element_type=F32)
    pos = jnp.where(hit, pos, -1.0)
    posx = jnp.concatenate(
        [jnp.broadcast_to(pos[e : e + 1, :], (CR, TOK)) for e in range(E)], axis=0
    )
    row16 = (sub % CR).astype(F32)
    picks = [(posx == row16 + float(CR * c)).astype(BF16) for c in range(CH)]

    own_term = None
    for dx in ORDER:
        t = term(dx, 0)
        lc[dx].wait_recv()
        t = t + lrecv[dx].astype(F32)
        if dx:
            tsend[dx] = t.astype(BF16)
            tc[dx - 1].start()
        else:
            own_term = t

    def id_copy(d):
        return rcopy(idrow_ref, ids.at[d], id_s.at[0], id_r.at[0], aa, ba_at(d))

    each_peer(lambda d: id_copy(d).start())
    ids[0] = idrow_ref[...]

    for c in loads[4:7]:
        c.wait()
    res = stream_v[...].astype(F32) + own_term
    for c in (1, 3, 2):
        tc[c - 1].wait_recv()
        res = res + trecv[c].astype(F32)
    resid[...] = res
    gain = gain_ref[...]
    sq = jnp.sum(res * res, axis=1, keepdims=True)
    stat_own[...] = jnp.transpose(jnp.broadcast_to(sq, (TOK, 128)))[0:8, :]
    stc = [
        rcopy(stat_own, stats.at[k], st_s.at[0], st_r.at[0], aa_at(k // 2, k % 2), ba)
        for k in range(1, 8)
    ]
    for c in stc:
        c.start()
    own_n = (res * gain).astype(BF16)
    nrm[xh] = own_n
    ncopy = rcopy(nrm.at[xh], nrm.at[xh], n_s.at[0], n_r.at[0], opp, ba)
    ncopy.start()

    grp = xp * 2 + core

    def a_copy(c, d):
        to = ba_at(d)
        return rcopy(
            outb.at[c, cols(div(to, 2), CR), cols(xh, SL)],
            xb.at[c, cols(ba, CR), cols(grp * 2 + xh, SL)],
            a_s.at[c, 0], a_r.at[c, 0], aa, to,
        )

    def o_copy(c, d):
        to = ba_at(d)
        return rcopy(
            outb.at[c, cols(div(to, 2), CR), cols(1 - xh, SL)],
            xb.at[c, cols(ba, CR), cols(grp * 2 + 1 - xh, SL)],
            a_s.at[c, 1], a_r.at[c, 1], aa, to,
        )

    def w_copy(c, d):
        to = ba_at(d)
        return rcopy(
            outb.at[c, cols(div(to, 2), CR), :],
            xb.at[c, cols(ba, CR), cols(grp, 2 * SL)],
            a_s.at[c, 0], a_r.at[c, 0], aa, to,
        )

    def fill(c, half):
        outb[c, :, cols(half, SL)] = jnp.dot(
            picks[c], nrm[half], preferred_element_type=F32
        ).astype(BF16)

    def send_rows(copy, c, at, width):
        each_peer(lambda d: copy(c, d).start())
        xb[c, cols(ba, CR), cols(grp * (2 * SL // width) + at, width)] = outb[
            c, cols(div(ba, 2), CR), cols(at, width)
        ]

    fill(0, xh)
    send_rows(a_copy, 0, xh, SL)
    total = stat_own[...]
    take(stats.at[pl.ds(1, 7)], st_r.at[0])
    for k in range(1, 8):
        total = total + stats[k]
    inv_row = lax.rsqrt(total * (1.0 / DIM) + EPS)

    e_row = lax.broadcasted_iota(jnp.int32, (8, TOK), 0)
    for e in range(E):
        rout[e] = jnp.where(e_row == 0, jnp.broadcast_to(pos[e : e + 1, :], (8, TOK)), inv_row)

    def rt_copy(d):
        to = ba_at(d)
        return rcopy(rout.at[div(to, 2)], routes.at[ba], rt_s.at[0], rt_r.at[0], aa, to)

    each_peer(lambda d: rt_copy(d).start())
    routes[ba] = rout[div(ba, 2)]
    fill(1, xh)
    send_rows(a_copy, 1, xh, SL)
    fill(2, xh)

    place = grp * 2 + xh
    xc, dc = [], []
    for c in range(CH):
        own = xb.at[c, :, cols(place, SL)]
        far = xb.at[c, :, cols(grp * 2 + 1 - xh, SL)]
        mine = xb.at[c, :, cols(grp, 2 * SL)]
        side = xb.at[c, :, cols((1 - xp) * 2 + core, 2 * SL)]
        xc.append(
            [
                rcopy(own, own, x_s.at[c, 0], x_r.at[c, 0], aa_at(1, 0), ba),
                rcopy(own, own, x_s.at[c, 1], x_r.at[c, 1], aa_at(3, 0), ba),
            ]
        )
        dc.append(
            [
                rcopy(r, r, d_s.at[c, i], d_r.at[c, i], sib, ba)
                for i, r in enumerate((own, far, side) if c < 2 else (mine, side))
            ]
        )

    half_ret = ret.at[0, pl.ds(0, ROWS - CR), pl.ds(0, SL)]
    full_ret = ret.at[0, pl.ds(0, ROWS - CR), :]
    half_rows = xb.at[0, pl.ds(0, ROWS - CR), pl.ds(0, SL)]
    full_rows = xb.at[0, pl.ds(0, ROWS - CR), pl.ds(0, 2 * SL)]

    def cross(c):
        for k in xc[c]:
            k.start()

    def arrive_own(c):
        take(half_rows, a_r.at[c, 0])
        if c == 0:
            cross(c)
        dc[c][0].start()

    def arrive_opp(c):
        take(half_rows, a_r.at[c, 1])
        dc[c][1].start()

    def arrive(c):
        take(full_rows, a_r.at[c, 0])
        for k in xc[c]:
            k.start()
        dc[c][0].start()

    def relay(c):
        for k in xc[c]:
            k.wait_recv()
        dc[c][-1].start()

    def scales(c):
        for s in range(16):
            r = routes[s]
            at = lax.broadcasted_iota(jnp.int32, (CR, TOK), 0).astype(F32) + float(CR * c)
            v = jnp.where(at == r[0:1, :], r[1:2, :], 0.0)
            scl[s * CR : (s + 1) * CR, :] = jnp.broadcast_to(
                jnp.sum(v, axis=1, keepdims=True), (CR, 128)
            )

    def activate(n, gu):
        g, u = gu[:, :128] * scl[...], gu[:, 128:] * scl[...]
        hid[:, n * 128 : (n + 1) * 128] = (g / (1.0 + jnp.exp(-g)) * u).astype(BF16)

    def part(n, which):
        return jnp.dot(
            xb[0, :, cols(which, 2048)], wgu[n, cols(which, 2048), :], preferred_element_type=F32
        )

    def gate_up(c):
        for n in range(NT):
            if c == 2 and n == 4:
                reduce_chips(0)
            activate(n, jnp.dot(xb[c], wgu[n], preferred_element_type=F32))

    def z_copy(c, dx):
        half = div(rem(x + dx, 4), 2)
        return rcopy(
            zsend.at[c, :, cols(half, SL)], zrecv.at[c, dx // 2], z_s.at[c, dx // 2],
            z_r.at[c, dx // 2], aa_at(dx, 0), ba,
        )

    zc = [{dx: z_copy(c, dx) for dx in (1, 3)} for c in range(CH)]
    yc = [
        [rcopy(ysend.at[c, i], yrecv.at[c, i], y_s.at[c, i], y_r.at[c, i], sib, ba) for i in range(2)]
        for c in range(CH)
    ]

    def b_copy(c, d):
        to = ba_at(d)
        return rcopy(
            rb.at[c, cols(to, CR), cols(xh, SL)], ret.at[c, cols(ba, CR), cols(xh, SL)],
            b_s.at[c, 0], b_r.at[c, 0], aa, to,
        )

    def q_copy(c, d):
        to = ba_at(d)
        return rcopy(
            rb.at[c, cols(to, CR), cols(1 - xh, SL)], ret.at[c, cols(ba, CR), cols(1 - xh, SL)],
            b_s.at[c, 1], b_r.at[c, 1], aa, to,
        )

    def v_copy(c, d):
        to = ba_at(d)
        return rcopy(
            rb.at[c, cols(to, CR), :], ret.at[c, cols(ba, CR), :],
            b_s.at[c, 0], b_r.at[c, 0], aa, to,
        )

    def down(group):
        return jnp.dot(hid[...], dv[group], preferred_element_type=F32)

    def project(c, before, after):
        for i, g in enumerate((1 - xp, xp)):
            ysend[c, i] = down(g * 2 + 1 - core).astype(BF16)
            yc[c][i].start()
        near[...] = down((1 - xp) * 2 + core)
        before()
        town[c] = down(xp * 2 + core)
        yc[c][0].wait_recv()
        zsend[c] = (near[...] + yrecv[c, 0].astype(F32)).astype(BF16)
        zc[c][1].start()
        zc[c][3].start()
        after()
        yc[c][1].wait_recv()
        v = town[c] + yrecv[c, 1].astype(F32)
        town[c] = v
        rb[c] = v.astype(BF16)
        if c:
            each_peer(lambda d: q_copy(c, d).start())
            ret[c, cols(ba, CR), cols(1 - xh, SL)] = rb[c, cols(ba, CR), cols(1 - xh, SL)]

    def reduce_chips(c):
        zc[c][1].wait_recv()
        zc[c][3].wait_recv()
        rb[c, :, cols(xh, SL)] = (
            town[c, :, cols(xh, SL)] + zrecv[c, 0].astype(F32) + zrecv[c, 1].astype(F32)
        ).astype(BF16)
        if c:
            each_peer(lambda d: b_copy(c, d).start())
            ret[c, cols(ba, CR), cols(xh, SL)] = rb[c, cols(ba, CR), cols(xh, SL)]
        else:
            each_peer(lambda d: v_copy(c, d).start())
            ret[c, cols(ba, CR), :] = rb[c, cols(ba, CR), :]

    def mix_weights():
        lg = lg_own[...]
        take(lgs.at[pl.ds(1, 7)], lg_r.at[0])
        for k in range(1, 8):
            lg = lg + lgs[k]
        l0 = jnp.sum(jnp.where(hit0, lg, 0.0), axis=0, keepdims=True)
        l1 = jnp.sum(jnp.where(hit1, lg, 0.0), axis=0, keepdims=True)
        w0 = 1.0 / (1.0 + jnp.exp(l1 - l0))
        w1 = 1.0 / (1.0 + jnp.exp(l0 - l1))
        return jnp.where(hit0, w0, 0.0) + jnp.where(hit1, w1, 0.0)

    def spread_weights(c, wx):
        w = jnp.where(posx == row16 + float(CR * c), wx, 0.0)
        hi = w.astype(BF16)
        lo = (w - hi.astype(F32)).astype(BF16)
        both = jnp.concatenate([hi, lo], axis=1)
        return jnp.concatenate(
            [both[(s // 2) * CR : (s // 2 + 1) * CR, :] for s in range(2 * E)], axis=0
        )

    def mix(c, wx, half):
        got = tdot(spread_weights(c, wx), ret[c, :, cols(half, SL)])
        got = got[:TOK, :] + got[TOK:, :]
        if c == 0:
            mx[half] = got
        else:
            mx[half] += got

    arrive_own(0)
    ncopy.wait_recv()
    fill(0, 1 - xh)
    send_rows(o_copy, 0, 1 - xh, SL)
    fill(1, 1 - xh)
    send_rows(o_copy, 1, 1 - xh, SL)
    fill(2, 1 - xh)
    inv = jnp.transpose(jnp.broadcast_to(inv_row[0:1, :], (128, TOK)))[:, 0:1]
    normed = (resid[...] * inv * gain).astype(BF16)
    lg_own[...] = ntdot(router_ref[...], normed)
    lgc = [
        rcopy(lg_own, lgs.at[k], lg_s.at[0], lg_r.at[0], aa_at(k // 2, k % 2), ba)
        for k in range(1, 8)
    ]
    for c in lgc:
        c.start()
    arrive_own(1)
    take(routes.at[pl.ds(0, 15)], rt_r.at[0])
    scales(0)
    send_rows(w_copy, 2, 0, 2 * SL)
    arrive_opp(0)
    cross(1)
    dc[0][0].wait_recv()
    dc[0][1].wait_recv()
    pltpu.make_async_copy(wgu, wgu, wsem.at[0]).wait()
    for n in range(5):
        acc[n] = part(n, xp)
    relay(0)
    for n in range(5, NT):
        acc[n] = part(n, xp)
    arrive_opp(1)
    dc[0][2].wait_recv()
    for n in range(NT):
        activate(n, acc[n] + part(n, 1 - xp))
    pltpu.make_async_copy(dv, dv, wsem.at[1]).wait()
    project(0, lambda: (arrive(2), relay(1)), lambda: None)
    scales(1)
    for k in dc[1]:
        k.wait_recv()
    gate_up(1)
    project(1, lambda: None, lambda: relay(2))
    scales(2)
    for k in dc[2][:2]:
        k.wait_recv()
    gate_up(2)
    wt = mix_weights()
    wx = jnp.concatenate(
        [jnp.broadcast_to(wt[e : e + 1, :], (CR, TOK)) for e in range(E)], axis=0
    )
    project(2, lambda: None, lambda: None)
    reduce_chips(1)
    take(full_ret, b_r.at[0, 0])
    mix(0, wx, 1 - xh)
    mix(0, wx, xh)

    take(ids.at[pl.ds(1, 15)], id_r.at[0])
    want = aa * 8 + lax.broadcasted_iota(jnp.int32, (8, TOK), 0)
    tally = jnp.zeros((8, TOK), F32)
    for d in range(16):
        tally = tally + (jnp.broadcast_to(ids[d], (8, TOK)) == want).astype(F32)
    cnt_ref[...] = jnp.broadcast_to(jnp.sum(tally, axis=1, keepdims=True), (8, TOK))

    take(half_ret, b_r.at[1, 1])
    mix(1, wx, 1 - xh)
    reduce_chips(2)
    take(half_ret, b_r.at[2, 1])
    mix(2, wx, 1 - xh)
    fsend[...] = mx[1 - xh].astype(BF16)
    fcopy = rcopy(fsend, frecv, f_s.at[0], f_r.at[0], opp, ba)
    fcopy.start()
    take(half_ret, b_r.at[1, 0])
    mix(1, wx, xh)
    take(half_ret, b_r.at[2, 0])
    mix(2, wx, xh)
    base = resid[...] + mx[xh]
    fcopy.wait_recv()
    out_ref[...] = (base + frecv[...].astype(F32)).astype(BF16)

    for c in lc + tc + [ncopy, fcopy]:
        c.wait_send()
    take(ids.at[pl.ds(1, 15)], id_s.at[0])
    take(stats.at[pl.ds(1, 7)], st_s.at[0])
    take(lgs.at[pl.ds(1, 7)], lg_s.at[0])
    take(routes.at[pl.ds(0, 15)], rt_s.at[0])
    for c in range(2):
        take(half_rows, a_s.at[c, 0])
        take(half_rows, a_s.at[c, 1])
    take(full_rows, a_s.at[2, 0])
    take(full_ret, b_s.at[0, 0])
    for c in (1, 2):
        take(half_ret, b_s.at[c, 0])
        take(half_ret, b_s.at[c, 1])
    for c in range(CH):
        for k in xc[c] + list(zc[c].values()) + dc[c] + yc[c]:
            k.wait_send()


def shards(
    head_outputs, stream, adapter_down_factors, adapter_up_factors, norm_gain_vector,
    router_matrix, token_adapter_index, token_expert_index, gate_weight, up_weight, down_weight,
):
    hbm = pl.BlockSpec(memory_space=pltpu.HBM)
    vmem = pl.BlockSpec(memory_space=pltpu.VMEM)
    V = pltpu.VMEM
    S = pltpu.SemaphoreType.DMA
    mixed, load = pl.pallas_call(
        kernel,
        out_shape=(
            jax.ShapeDtypeStruct((TOK, SL), BF16),
            jax.ShapeDtypeStruct((8, TOK), F32),
        ),
        in_specs=[hbm] * 11,
        out_specs=(vmem, vmem),
        scratch_shapes=[
            V((TOK, DIM), BF16),
            V((DIM, 128), BF16),
            V((128, DIM), BF16),
            V((TOK, SL), BF16),
            V((1, SL), F32),
            V((E, SL), BF16),
            V((1, TOK), jnp.int32),
            V((2, TOK), jnp.int32),
            V((NT, DIM, 256), BF16),
            V((4, FFD, 2 * SL), BF16),
            V((4, TOK, SL), BF16),
            V((4, TOK, SL), BF16),
            V((4, TOK, SL), BF16),
            V((4, TOK, SL), BF16),
            V((8, 8, TOK), F32),
            V((8, TOK), F32),
            V((8, E, TOK), F32),
            V((E, TOK), F32),
            V((16, 1, TOK), jnp.int32),
            V((E, 8, TOK), F32),
            V((16, 8, TOK), F32),
            V((ROWS, 128), F32),
            V((2, TOK, SL), BF16),
            V((CH, E * CR, 2 * SL), BF16),
            V((CH, ROWS, DIM), BF16),
            V((ROWS, FFD), BF16),
            V((CH, 2, ROWS, 2 * SL), BF16),
            V((CH, 2, ROWS, 2 * SL), BF16),
            V((ROWS, 2 * SL), F32),
            V((CH, ROWS, 2 * SL), F32),
            V((CH, ROWS, 2 * SL), BF16),
            V((CH, 2, ROWS, SL), BF16),
            V((CH, ROWS, 2 * SL), BF16),
            V((CH, ROWS, 2 * SL), BF16),
            V((2, TOK, SL), F32),
            V((TOK, SL), BF16),
            V((TOK, SL), BF16),
            V((TOK, SL), F32),
            V((NT, ROWS, 256), F32),
            S((8,)), S((2,)),
            S((4,)), S((4,)), S((4,)), S((4,)), S((1,)), S((1,)), S((1,)), S((1,)),
            S((1,)), S((1,)), S((1,)), S((1,)),
            S((1,)), S((1,)),
            S((CH, 2)), S((CH, 2)),
            S((CH, 2)), S((CH, 2)), S((CH, 3)), S((CH, 3)),
            S((CH, 2)), S((CH, 2)),
            S((CH, 2)), S((CH, 2)),
            S((CH, 2)), S((CH, 2)),
            S((1,)), S((1,)),
        ],
        compiler_params=pltpu.CompilerParams(
            collective_id=0, has_side_effects=True, vmem_limit_bytes=56_000_000
        ),
    )(*[pltpu.with_memory_space_constraint(a, pltpu.HBM) for a in (
        head_outputs, stream, adapter_down_factors, adapter_up_factors,
        norm_gain_vector.reshape(1, DIM), router_matrix.T,
        token_adapter_index.reshape(1, TOK),
        token_expert_index.T, gate_weight[0], up_weight[0], down_weight[0],
    )])
    return mixed, load[:, 0]


def solution(mesh):
    in_specs = (
        P("ba", None), P("ba", None), P(None, "aa"), P("aa", None), P(), P(), P("ba"),
        P("ba", None), P("ba", None, "aa"), P("ba", None, "aa"), P("ba", "aa", None),
    )
    out_specs = (P("ba", "aa"), P("aa"))
    return jax.shard_map(shards, mesh=mesh, in_specs=in_specs, out_specs=out_specs, check_vma=False)
```

time: 97.5 us -> 80.8 us (0.83)
  Pallas kernels: 92.3 us -> 78.8 us
  local copies, waits for them, and re-layouts: 4.26 us -> 1.28 us
    pallas_call x1, Pallas kernels: 92.3 us -> 78.8 us  [shards(): pl.pallas_call(kernel, out_shape=(jax.ShapeDtypeStruct((TOK, SL), BF16),...]
    reshape x1 -> x0, local copies, waits for them, and re-layouts: 1.39 us -> none  [shards(): token_adapter_index.reshape(TOK, 1)]
where the time goes in v3:
time: 80.8 us; the launch traced here: 80.7 us
  Pallas kernels  78.8 us (98%)
  local copies, waits for them, and re-layouts  1.28 us (2%)
    pallas_call x1, Pallas kernels, shards(): pl.pallas_call(kernel, out_shape=(jax.ShapeDtypeStruct((TOK, SL), BF16),...  78.8 us

profile of v3, /device:TPU:0, one launch (start us, length us, event | category | flops | bytes accessed | tf_op | source)
XLA Modules:
  0.0 80.7 jit_solution(2831811975840374927)
XLA Ops:
  0.6 78.8 %shard_map.122 = (bf16[128,512]{1,0:T(8,128)(2,1)S(1)}, f32[8,128]{1,0:T(8,128)S(1)}) custom-call(bf16[128,4096]{1,0:T(8,128)(2,1)} %head_h.1, bf16[128,4096]{1,0:T(8,128)(2,1)} %stream_h.1, bf16[4096,128]{1,0:T(8,128)(2,1)} %down_h.1, bf16[128,4096]{1,0:T(8,128)(2,1)} %up_h.1, f32[1,4096]{1,0:T(1,128)} %bitcast.11, bf16[8,4096]{1,0:T(8,128)(2,1)} %bitcast.10, ...), custom_call_target="tpu_custom_call" | custom-call | tf_op jit(solution)/shard_map/pallas_call | solution.py:541
  79.4 0.6 slice_reduce_fusion
  80.0 0.7 copy.14

commit v4 on v3

--- a/solution.py
+++ b/solution.py
@@ -15,6 +15,7 @@
 CR = 16
 ROWS = 256
 SL = 512
+HS = SL // 2
 NT = FFD // 128
 EPS = 1e-05
 F32 = jnp.float32
@@ -55,8 +56,10 @@
     def aa_at(dx, dc):
         return rem(x + dx, 4) * 2 + rem(core + dc, 2)
 
+    peers = [rem(z + d // 4, 4) * 4 + rem(y + d % 4, 4) for d in range(16)]
+
     def ba_at(d):
-        return rem(z + div(d, 4), 4) * 4 + rem(y + rem(d, 4), 4)
+        return peers[d]
 
     def take(ref, sem):
         pltpu.make_async_copy(ref, ref, sem).wait()
@@ -71,11 +74,8 @@
         return pl.ds(pl.multiple_of(i * width, width), width)
 
     def each_peer(body):
-        def step(d, carry):
+        for d in range(1, 16):
             body(d)
-            return carry
-
-        lax.fori_loop(1, 16, step, 0)
 
     sib = aa_at(0, 1)
     opp = aa_at(2, 0)
@@ -281,8 +281,8 @@
             ]
         )
 
+    quarter_ret = ret.at[0, pl.ds(0, ROWS - CR), pl.ds(0, HS)]
     half_ret = ret.at[0, pl.ds(0, ROWS - CR), pl.ds(0, SL)]
-    full_ret = ret.at[0, pl.ds(0, ROWS - CR), :]
     half_rows = xb.at[0, pl.ds(0, ROWS - CR), pl.ds(0, SL)]
     full_rows = xb.at[0, pl.ds(0, ROWS - CR), pl.ds(0, 2 * SL)]
 
@@ -324,86 +324,85 @@
         g, u = gu[:, :128] * scl[...], gu[:, 128:] * scl[...]
         hid[:, n * 128 : (n + 1) * 128] = (g / (1.0 + jnp.exp(-g)) * u).astype(BF16)
 
-    def part(n, which):
-        return jnp.dot(
-            xb[0, :, cols(which, 2048)], wgu[n, cols(which, 2048), :], preferred_element_type=F32
+    def part(n, *blocks):
+        return sum(
+            jnp.dot(xb[0, :, k], wgu[n, k, :], preferred_element_type=F32) for k in blocks
         )
 
     def gate_up(c):
         for n in range(NT):
-            if c == 2 and n == 4:
+            if n == 6 and c == 2:
                 reduce_chips(0)
             activate(n, jnp.dot(xb[c], wgu[n], preferred_element_type=F32))
 
-    def z_copy(c, dx):
-        half = div(rem(x + dx, 4), 2)
+    def z_copy(c, dx, h):
+        half, i = div(rem(x + dx, 4), 2), dx // 2
         return rcopy(
-            zsend.at[c, :, cols(half, SL)], zrecv.at[c, dx // 2], z_s.at[c, dx // 2],
-            z_r.at[c, dx // 2], aa_at(dx, 0), ba,
-        )
-
-    zc = [{dx: z_copy(c, dx) for dx in (1, 3)} for c in range(CH)]
+            zsend.at[c, :, cols(half * 2 + h, HS)], zrecv.at[c, i, :, h * HS : (h + 1) * HS],
+            z_s.at[c, i + 2 * h], z_r.at[c, i + 2 * h], aa_at(dx, 0), ba,
+        )
+
+    zc = [[[z_copy(c, dx, h) for dx in (1, 3)] for h in range(2)] for c in range(CH)]
     yc = [
         [rcopy(ysend.at[c, i], yrecv.at[c, i], y_s.at[c, i], y_r.at[c, i], sib, ba) for i in range(2)]
         for c in range(CH)
     ]
 
-    def b_copy(c, d):
+    def b_copy(c, d, h):
         to = ba_at(d)
+        at = cols(xh * 2 + h, HS)
         return rcopy(
-            rb.at[c, cols(to, CR), cols(xh, SL)], ret.at[c, cols(ba, CR), cols(xh, SL)],
-            b_s.at[c, 0], b_r.at[c, 0], aa, to,
+            rb.at[c, cols(to, CR), at], ret.at[c, cols(ba, CR), at],
+            b_s.at[c, h], b_r.at[c, h], aa, to,
         )
 
     def q_copy(c, d):
         to = ba_at(d)
         return rcopy(
             rb.at[c, cols(to, CR), cols(1 - xh, SL)], ret.at[c, cols(ba, CR), cols(1 - xh, SL)],
-            b_s.at[c, 1], b_r.at[c, 1], aa, to,
-        )
-
-    def v_copy(c, d):
-        to = ba_at(d)
-        return rcopy(
-            rb.at[c, cols(to, CR), :], ret.at[c, cols(ba, CR), :],
-            b_s.at[c, 0], b_r.at[c, 0], aa, to,
+            b_s.at[c, 2], b_r.at[c, 2], aa, to,
         )
 
     def down(group):
         return jnp.dot(hid[...], dv[group], preferred_element_type=F32)
 
-    def project(c, before, after):
-        for i, g in enumerate((1 - xp, xp)):
-            ysend[c, i] = down(g * 2 + 1 - core).astype(BF16)
-            yc[c][i].start()
+    def project(c, before_last):
+        ysend[c, 0] = down((1 - xp) * 2 + 1 - core).astype(BF16)
+        yc[c][0].start()
+        ysend[c, 1] = down(xp * 2 + 1 - core).astype(BF16)
+        yc[c][1].start()
         near[...] = down((1 - xp) * 2 + core)
-        before()
+        before_last()
         town[c] = down(xp * 2 + core)
+
+    def pair_near(c):
         yc[c][0].wait_recv()
         zsend[c] = (near[...] + yrecv[c, 0].astype(F32)).astype(BF16)
-        zc[c][1].start()
-        zc[c][3].start()
-        after()
+
+    def pair_own(c):
         yc[c][1].wait_recv()
         v = town[c] + yrecv[c, 1].astype(F32)
         town[c] = v
         rb[c] = v.astype(BF16)
-        if c:
-            each_peer(lambda d: q_copy(c, d).start())
-            ret[c, cols(ba, CR), cols(1 - xh, SL)] = rb[c, cols(ba, CR), cols(1 - xh, SL)]
+
+    def send_near(c):
+        for k in zc[c][0] + zc[c][1]:
+            k.start()
+
+    def send_far(c):
+        each_peer(lambda d: q_copy(c, d).start())
+        ret[c, cols(ba, CR), cols(1 - xh, SL)] = rb[c, cols(ba, CR), cols(1 - xh, SL)]
 
     def reduce_chips(c):
-        zc[c][1].wait_recv()
-        zc[c][3].wait_recv()
-        rb[c, :, cols(xh, SL)] = (
-            town[c, :, cols(xh, SL)] + zrecv[c, 0].astype(F32) + zrecv[c, 1].astype(F32)
-        ).astype(BF16)
-        if c:
-            each_peer(lambda d: b_copy(c, d).start())
-            ret[c, cols(ba, CR), cols(xh, SL)] = rb[c, cols(ba, CR), cols(xh, SL)]
-        else:
-            each_peer(lambda d: v_copy(c, d).start())
-            ret[c, cols(ba, CR), :] = rb[c, cols(ba, CR), :]
+        for h in range(2):
+            for k in zc[c][h]:
+                k.wait_recv()
+            at, here = cols(xh * 2 + h, HS), slice(h * HS, (h + 1) * HS)
+            rb[c, :, at] = (
+                town[c, :, at] + zrecv[c, 0, :, here].astype(F32) + zrecv[c, 1, :, here].astype(F32)
+            ).astype(BF16)
+            each_peer(lambda d: b_copy(c, d, h).start())
+            ret[c, cols(ba, CR), at] = rb[c, cols(ba, CR), at]
 
     def mix_weights():
         lg = lg_own[...]
@@ -433,10 +432,10 @@
         else:
             mx[half] += got
 
-    arrive_own(0)
     ncopy.wait_recv()
     fill(0, 1 - xh)
     send_rows(o_copy, 0, 1 - xh, SL)
+    arrive_own(0)
     fill(1, 1 - xh)
     send_rows(o_copy, 1, 1 - xh, SL)
     fill(2, 1 - xh)
@@ -449,31 +448,41 @@
     ]
     for c in lgc:
         c.start()
+    own_k = (cols(xp * 4 + xh, SL), cols(xp * 4 + 2 + xh, SL))
+    far_k = (cols(xp * 4 + 1 - xh, SL), cols(xp * 4 + 3 - xh, SL))
+    dc[0][0].wait_recv()
+    pltpu.make_async_copy(wgu, wgu, wsem.at[0]).wait()
+    for n in range(NT):
+        acc[n] = part(n, *own_k)
     arrive_own(1)
+    cross(1)
     take(routes.at[pl.ds(0, 15)], rt_r.at[0])
     scales(0)
     send_rows(w_copy, 2, 0, 2 * SL)
     arrive_opp(0)
-    cross(1)
-    dc[0][0].wait_recv()
+    relay(0)
     dc[0][1].wait_recv()
-    pltpu.make_async_copy(wgu, wgu, wsem.at[0]).wait()
-    for n in range(5):
-        acc[n] = part(n, xp)
-    relay(0)
-    for n in range(5, NT):
-        acc[n] = part(n, xp)
+    for n in range(NT):
+        acc[n] += part(n, *far_k)
     arrive_opp(1)
     dc[0][2].wait_recv()
     for n in range(NT):
-        activate(n, acc[n] + part(n, 1 - xp))
+        activate(n, acc[n] + part(n, cols(1 - xp, 2048)))
     pltpu.make_async_copy(dv, dv, wsem.at[1]).wait()
-    project(0, lambda: (arrive(2), relay(1)), lambda: None)
+    project(0, lambda: (relay(1), arrive(2)))
+    pair_near(0)
+    send_near(0)
+    pair_own(0)
+    send_far(0)
     scales(1)
     for k in dc[1]:
         k.wait_recv()
     gate_up(1)
-    project(1, lambda: None, lambda: relay(2))
+    project(1, lambda: relay(2))
+    pair_near(1)
+    send_near(1)
+    pair_own(1)
+    send_far(1)
     scales(2)
     for k in dc[2][:2]:
         k.wait_recv()
@@ -482,12 +491,10 @@
     wx = jnp.concatenate(
         [jnp.broadcast_to(wt[e : e + 1, :], (CR, TOK)) for e in range(E)], axis=0
     )
-    project(2, lambda: None, lambda: None)
+    project(2, lambda: (pair_near(2), send_near(2)))
+    pair_own(2)
+    send_far(2)
     reduce_chips(1)
-    take(full_ret, b_r.at[0, 0])
-    mix(0, wx, 1 - xh)
-    mix(0, wx, xh)
-
     take(ids.at[pl.ds(1, 15)], id_r.at[0])
     want = aa * 8 + lax.broadcasted_iota(jnp.int32, (8, TOK), 0)
     tally = jnp.zeros((8, TOK), F32)
@@ -495,17 +502,23 @@
         tally = tally + (jnp.broadcast_to(ids[d], (8, TOK)) == want).astype(F32)
     cnt_ref[...] = jnp.broadcast_to(jnp.sum(tally, axis=1, keepdims=True), (8, TOK))
 
-    take(half_ret, b_r.at[1, 1])
-    mix(1, wx, 1 - xh)
+    for c in (0, 1):
+        take(half_ret, b_r.at[c, 2])
+        mix(c, wx, 1 - xh)
+    take(quarter_ret, b_r.at[0, 0])
+    take(quarter_ret, b_r.at[0, 1])
+    mix(0, wx, xh)
     reduce_chips(2)
-    take(half_ret, b_r.at[2, 1])
+    take(half_ret, b_r.at[2, 2])
     mix(2, wx, 1 - xh)
     fsend[...] = mx[1 - xh].astype(BF16)
     fcopy = rcopy(fsend, frecv, f_s.at[0], f_r.at[0], opp, ba)
     fcopy.start()
-    take(half_ret, b_r.at[1, 0])
+    take(quarter_ret, b_r.at[1, 0])
+    take(quarter_ret, b_r.at[1, 1])
     mix(1, wx, xh)
-    take(half_ret, b_r.at[2, 0])
+    take(quarter_ret, b_r.at[2, 0])
+    take(quarter_ret, b_r.at[2, 1])
     mix(2, wx, xh)
     base = resid[...] + mx[xh]
     fcopy.wait_recv()
@@ -521,12 +534,12 @@
         take(half_rows, a_s.at[c, 0])
         take(half_rows, a_s.at[c, 1])
     take(full_rows, a_s.at[2, 0])
-    take(full_ret, b_s.at[0, 0])
-    for c in (1, 2):
-        take(half_ret, b_s.at[c, 0])
-        take(half_ret, b_s.at[c, 1])
     for c in range(CH):
-        for k in xc[c] + list(zc[c].values()) + dc[c] + yc[c]:
+        take(quarter_ret, b_s.at[c, 0])
+        take(quarter_ret, b_s.at[c, 1])
+        take(half_ret, b_s.at[c, 2])
+    for c in range(CH):
+        for k in xc[c] + zc[c][0] + zc[c][1] + dc[c] + yc[c]:
             k.wait_send()
 
 
@@ -593,8 +606,8 @@
             S((CH, 2)), S((CH, 2)),
             S((CH, 2)), S((CH, 2)), S((CH, 3)), S((CH, 3)),
             S((CH, 2)), S((CH, 2)),
-            S((CH, 2)), S((CH, 2)),
-            S((CH, 2)), S((CH, 2)),
+            S((CH, 4)), S((CH, 4)),
+            S((CH, 3)), S((CH, 3)),
             S((1,)), S((1,)),
         ],
         compiler_params=pltpu.CompilerParams(

time: 80.8 us -> 77.9 us (0.964)
  Pallas kernels: 78.8 us -> 75.6 us
    pallas_call x1, Pallas kernels: 78.8 us -> 75.6 us  [shards(): pl.pallas_call(kernel, out_shape=(jax.ShapeDtypeStruct((TOK, SL), BF16),...]
where the time goes in v4:
time: 77.9 us; the launch traced here: 77.6 us
  Pallas kernels  75.6 us (97%)
  local copies, waits for them, and re-layouts  1.28 us (2%)
    pallas_call x1, Pallas kernels, shards(): pl.pallas_call(kernel, out_shape=(jax.ShapeDtypeStruct((TOK, SL), BF16),...  75.6 us

profile of v4, /device:TPU:0, one launch (start us, length us, event | category | flops | bytes accessed | tf_op | source)
XLA Modules:
  0.0 77.6 jit_solution(6350433114553290955)
XLA Ops:
  0.6 75.6 %shard_map.122 = (bf16[128,512]{1,0:T(8,128)(2,1)S(1)}, f32[8,128]{1,0:T(8,128)S(1)}) custom-call(bf16[128,4096]{1,0:T(8,128)(2,1)} %head_h.1, bf16[128,4096]{1,0:T(8,128)(2,1)} %stream_h.1, bf16[4096,128]{1,0:T(8,128)(2,1)} %down_h.1, bf16[128,4096]{1,0:T(8,128)(2,1)} %up_h.1, f32[1,4096]{1,0:T(1,128)} %bitcast.11, bf16[8,4096]{1,0:T(8,128)(2,1)} %bitcast.10, ...), custom_call_target="tpu_custom_call" | custom-call | tf_op jit(solution)/shard_map/pallas_call | solution.py:554
  76.3 0.6 slice_reduce_fusion
  76.9 0.7 copy.14

commit v5 on v4

--- a/solution.py
+++ b/solution.py
@@ -114,6 +114,34 @@
     rank = jnp.where(idcol == (aa * 8 + lane // RANK).astype(F32), rank, 0.0).astype(BF16)
     loads[2].wait()
 
+    def term(dx, dc):
+        part = up_v[:, cols(aa_at(dx, dc), SL)]
+        return 2.0 * jnp.dot(rank, part, preferred_element_type=F32)
+
+    ORDER = (2, 1, 3, 0)
+    for dx in ORDER:
+        lsend[dx] = term(dx, 1).astype(BF16)
+
+    pl.semaphore_wait(barrier, 22)
+    lc = [rcopy(lsend.at[i], lrecv.at[i], l_s.at[i], l_r.at[i], sib, ba) for i in range(4)]
+    tc = [
+        rcopy(tsend.at[i], trecv.at[i], t_s.at[i], t_r.at[i], aa_at(i, 0), ba)
+        for i in range(1, 4)
+    ]
+    for dx in ORDER:
+        lc[dx].start()
+
+    own_term = None
+    for dx in ORDER:
+        t = term(dx, 0)
+        lc[dx].wait_recv()
+        t = t + lrecv[dx].astype(F32)
+        if dx:
+            tsend[dx] = t.astype(BF16)
+            tc[dx - 1].start()
+        else:
+            own_term = t
+
     def load_w(n, carry):
         for f in range(8):
             p = place_of(f)
@@ -133,22 +161,11 @@
             wsem.at[1],
         ).start()
 
-    def term(dx, dc):
-        part = up_v[:, cols(aa_at(dx, dc), SL)]
-        return 2.0 * jnp.dot(rank, part, preferred_element_type=F32)
-
-    ORDER = (2, 1, 3, 0)
-    for dx in ORDER:
-        lsend[dx] = term(dx, 1).astype(BF16)
-
-    pl.semaphore_wait(barrier, 22)
-    lc = [rcopy(lsend.at[i], lrecv.at[i], l_s.at[i], l_r.at[i], sib, ba) for i in range(4)]
-    tc = [
-        rcopy(tsend.at[i], trecv.at[i], t_s.at[i], t_r.at[i], aa_at(i, 0), ba)
-        for i in range(1, 4)
-    ]
-    for dx in ORDER:
-        lc[dx].start()
+    def id_copy(d):
+        return rcopy(idrow_ref, ids.at[d], id_s.at[0], id_r.at[0], aa, ba_at(d))
+
+    each_peer(lambda d: id_copy(d).start())
+    ids[0] = idrow_ref[...]
 
     loads[7].wait()
     ex0, ex1 = ex_ref[0:1, :], ex_ref[1:2, :]
@@ -164,23 +181,6 @@
     row16 = (sub % CR).astype(F32)
     picks = [(posx == row16 + float(CR * c)).astype(BF16) for c in range(CH)]
 
-    own_term = None
-    for dx in ORDER:
-        t = term(dx, 0)
-        lc[dx].wait_recv()
-        t = t + lrecv[dx].astype(F32)
-        if dx:
-            tsend[dx] = t.astype(BF16)
-            tc[dx - 1].start()
-        else:
-            own_term = t
-
-    def id_copy(d):
-        return rcopy(idrow_ref, ids.at[d], id_s.at[0], id_r.at[0], aa, ba_at(d))
-
-    each_peer(lambda d: id_copy(d).start())
-    ids[0] = idrow_ref[...]
-
     for c in loads[4:7]:
         c.wait()
     res = stream_v[...].astype(F32) + own_term
@@ -189,6 +189,50 @@
         res = res + trecv[c].astype(F32)
     resid[...] = res
     gain = gain_ref[...]
+    own_n = (res * gain).astype(BF16)
+    nrm[xh] = own_n
+    ncopy = rcopy(nrm.at[xh], nrm.at[xh], n_s.at[0], n_r.at[0], opp, ba)
+    ncopy.start()
+
+    grp = xp * 2 + core
+
+    def a_copy(c, d):
+        to = ba_at(d)
+        return rcopy(
+            outb.at[c, cols(div(to, 2), CR), cols(xh, SL)],
+            xb.at[c, cols(ba, CR), cols(grp * 2 + xh, SL)],
+            a_s.at[c, 0], a_r.at[c, 0], aa, to,
+        )
+
+    def o_copy(c, d):
+        to = ba_at(d)
+        return rcopy(
+            outb.at[c, cols(div(to, 2), CR), cols(1 - xh, SL)],
+            xb.at[c, cols(ba, CR), cols(grp * 2 + 1 - xh, SL)],
+            a_s.at[c, 1], a_r.at[c, 1], aa, to,
+        )
+
+    def w_copy(c, d):
+        to = ba_at(d)
+        return rcopy(
+            outb.at[c, cols(div(to, 2), CR), :],
+            xb.at[c, cols(ba, CR), cols(grp, 2 * SL)],
+            a_s.at[c, 0], a_r.at[c, 0], aa, to,
+        )
+
+    def fill(c, half):
+        outb[c, :, cols(half, SL)] = jnp.dot(
+            picks[c], nrm[half], preferred_element_type=F32
+        ).astype(BF16)
+
+    def send_rows(copy, c, at, width):
+        each_peer(lambda d: copy(c, d).start())
+        xb[c, cols(ba, CR), cols(grp * (2 * SL // width) + at, width)] = outb[
+            c, cols(div(ba, 2), CR), cols(at, width)
+        ]
+
+    fill(0, xh)
+    send_rows(a_copy, 0, xh, SL)
     sq = jnp.sum(res * res, axis=1, keepdims=True)
     stat_own[...] = jnp.transpose(jnp.broadcast_to(sq, (TOK, 128)))[0:8, :]
     stc = [
@@ -197,66 +241,6 @@
     ]
     for c in stc:
         c.start()
-    own_n = (res * gain).astype(BF16)
-    nrm[xh] = own_n
-    ncopy = rcopy(nrm.at[xh], nrm.at[xh], n_s.at[0], n_r.at[0], opp, ba)
-    ncopy.start()
-
-    grp = xp * 2 + core
-
-    def a_copy(c, d):
-        to = ba_at(d)
-        return rcopy(
-            outb.at[c, cols(div(to, 2), CR), cols(xh, SL)],
-            xb.at[c, cols(ba, CR), cols(grp * 2 + xh, SL)],
-            a_s.at[c, 0], a_r.at[c, 0], aa, to,
-        )
-
-    def o_copy(c, d):
-        to = ba_at(d)
-        return rcopy(
-            outb.at[c, cols(div(to, 2), CR), cols(1 - xh, SL)],
-            xb.at[c, cols(ba, CR), cols(grp * 2 + 1 - xh, SL)],
-            a_s.at[c, 1], a_r.at[c, 1], aa, to,
-        )
-
-    def w_copy(c, d):
-        to = ba_at(d)
-        return rcopy(
-            outb.at[c, cols(div(to, 2), CR), :],
-            xb.at[c, cols(ba, CR), cols(grp, 2 * SL)],
-            a_s.at[c, 0], a_r.at[c, 0], aa, to,
-        )
-
-    def fill(c, half):
-        outb[c, :, cols(half, SL)] = jnp.dot(
-            picks[c], nrm[half], preferred_element_type=F32
-        ).astype(BF16)
-
-    def send_rows(copy, c, at, width):
-        each_peer(lambda d: copy(c, d).start())
-        xb[c, cols(ba, CR), cols(grp * (2 * SL // width) + at, width)] = outb[
-            c, cols(div(ba, 2), CR), cols(at, width)
-        ]
-
-    fill(0, xh)
-    send_rows(a_copy, 0, xh, SL)
-    total = stat_own[...]
-    take(stats.at[pl.ds(1, 7)], st_r.at[0])
-    for k in range(1, 8):
-        total = total + stats[k]
-    inv_row = lax.rsqrt(total * (1.0 / DIM) + EPS)
-
-    e_row = lax.broadcasted_iota(jnp.int32, (8, TOK), 0)
-    for e in range(E):
-        rout[e] = jnp.where(e_row == 0, jnp.broadcast_to(pos[e : e + 1, :], (8, TOK)), inv_row)
-
-    def rt_copy(d):
-        to = ba_at(d)
-        return rcopy(rout.at[div(to, 2)], routes.at[ba], rt_s.at[0], rt_r.at[0], aa, to)
-
-    each_peer(lambda d: rt_copy(d).start())
-    routes[ba] = rout[div(ba, 2)]
     fill(1, xh)
     send_rows(a_copy, 1, xh, SL)
     fill(2, xh)
@@ -436,6 +420,22 @@
     fill(0, 1 - xh)
     send_rows(o_copy, 0, 1 - xh, SL)
     arrive_own(0)
+    total = stat_own[...]
+    take(stats.at[pl.ds(1, 7)], st_r.at[0])
+    for k in range(1, 8):
+        total = total + stats[k]
+    inv_row = lax.rsqrt(total * (1.0 / DIM) + EPS)
+
+    e_row = lax.broadcasted_iota(jnp.int32, (8, TOK), 0)
+    for e in range(E):
+        rout[e] = jnp.where(e_row == 0, jnp.broadcast_to(pos[e : e + 1, :], (8, TOK)), inv_row)
+
+    def rt_copy(d):
+        to = ba_at(d)
+        return rcopy(rout.at[div(to, 2)], routes.at[ba], rt_s.at[0], rt_r.at[0], aa, to)
+
+    each_peer(lambda d: rt_copy(d).start())
+    routes[ba] = rout[div(ba, 2)]
     fill(1, 1 - xh)
     send_rows(o_copy, 1, 1 - xh, SL)
     fill(2, 1 - xh)

time: 77.9 us -> 75.8 us (0.973)
  Pallas kernels: 75.6 us -> 73.8 us
    pallas_call x1, Pallas kernels: 75.6 us -> 73.8 us  [shards(): pl.pallas_call(kernel, out_shape=(jax.ShapeDtypeStruct((TOK, SL), BF16),...]
where the time goes in v5:
time: 75.8 us; the launch traced here: 75.7 us
  Pallas kernels  73.8 us (97%)
  local copies, waits for them, and re-layouts  1.28 us (2%)
    pallas_call x1, Pallas kernels, shards(): pl.pallas_call(kernel, out_shape=(jax.ShapeDtypeStruct((TOK, SL), BF16),...  73.8 us

profile of v5, /device:TPU:0, one launch (start us, length us, event | category | flops | bytes accessed | tf_op | source)
XLA Modules:
  0.0 75.7 jit_solution(17553652408940977271)
XLA Ops:
  0.6 73.8 %shard_map.122 = (bf16[128,512]{1,0:T(8,128)(2,1)S(1)}, f32[8,128]{1,0:T(8,128)S(1)}) custom-call(bf16[128,4096]{1,0:T(8,128)(2,1)} %head_h.1, bf16[128,4096]{1,0:T(8,128)(2,1)} %stream_h.1, bf16[4096,128]{1,0:T(8,128)(2,1)} %down_h.1, bf16[128,4096]{1,0:T(8,128)(2,1)} %up_h.1, f32[1,4096]{1,0:T(1,128)} %bitcast.11, bf16[8,4096]{1,0:T(8,128)(2,1)} %bitcast.10, ...), custom_call_target="tpu_custom_call" | custom-call | tf_op jit(solution)/shard_map/pallas_call | solution.py:554
  74.4 0.6 slice_reduce_fusion
  75.0 0.7 copy.14
